TPU v7x, 32 devices: a 4x2x2 block of a 4x4x8 slice. The times are simulated.
32 devices in a mesh: dp: 4 (over y, z), ep: 8 (over x, core).
Axes of the slice: x: 4, y: 2, z: 2, core: 2. Of those that a mesh axis runs over, the one named last changes fastest.
The devices are a block of a 4x4x8 slice.
Arguments:
- tokens: bfloat16 [32768, 2048], P(('dp', 'ep')), parts along dimension 0
- w_router: bfloat16 [2048, 64], replicated
- expert_ids: int32 [32768, 6], P(('dp', 'ep')), parts along dimension 0
- w_gate: bfloat16 [64, 2048, 1408], P('ep')
- w_up: bfloat16 [64, 2048, 1408], P('ep')
- w_down: bfloat16 [64, 1408, 2048], P('ep')
- shared_gate: bfloat16 [2048, 2816], replicated
- shared_up: bfloat16 [2048, 2816], replicated
- shared_down: bfloat16 [2816, 2048], replicated
Outputs:
- output: bfloat16 [32768, 2048], P(('dp', 'ep')), parts along dimension 0
There are 4 independent parts. A program takes and returns all parts, laid end to end along the dimension named above; an argument that names none is the same for every part.
All inputs are finite; a program needn't handle non-finite values.
Results may differ from a plain program's by a relative error of at most 0.00812481.
Values are sent between devices in bfloat16 or wider.
A program may use at most 768 MiB of HBM per device.

v0:
```python
import jax
import jax.numpy as jnp
from jax import lax
from jax.sharding import PartitionSpec as P


def capacity_of(tok_dev, top_k, num_exp):
    base_load = tok_dev * top_k // num_exp
    return base_load + base_load // 2 + min(tok_dev * top_k % num_exp, 1)


def gate_values(tok_rows, w_router, ids_loc):
    logits = jnp.dot(tok_rows, w_router, preferred_element_type=jnp.float32)
    picked = jnp.take_along_axis(logits, ids_loc, axis=1)
    return jax.nn.softmax(picked, axis=-1)


def dispatch_tables(ids_loc, num_exp, capacity):
    tok_dev, top_k = ids_loc.shape
    num_pairs = tok_dev * top_k
    flat_ids = ids_loc.reshape(-1)
    sort_order = jnp.argsort(flat_ids, stable=True)
    sorted_ids = flat_ids[sort_order]
    counts = jnp.bincount(flat_ids, length=num_exp)
    starts = jnp.cumsum(counts) - counts
    pair_range = jnp.arange(num_pairs, dtype=jnp.int32)
    slot_sorted = sorted_ids * capacity + pair_range - starts[sorted_ids]
    slot_pos = jnp.zeros((num_pairs,), jnp.int32).at[sort_order].set(slot_sorted)
    row_range = jnp.arange(capacity, dtype=jnp.int32)
    src_pos = jnp.minimum(starts[:, None] + row_range[None, :], num_pairs - 1)
    pair_id = sort_order[src_pos]
    buf_tok = jnp.where(row_range[None, :] < counts[:, None], pair_id // top_k, tok_dev)
    return slot_pos.reshape(tok_dev, top_k), buf_tok


def expert_mlp(rows_in, w_gate, w_up, w_down):
    gate_act = jnp.einsum('ecd,edf->ecf', rows_in, w_gate, preferred_element_type=jnp.float32)
    up_act = jnp.einsum('ecd,edf->ecf', rows_in, w_up, preferred_element_type=jnp.float32)
    hidden = (jax.nn.silu(gate_act) * up_act).astype(jnp.bfloat16)
    return jnp.einsum('ecf,efd->ecd', hidden, w_down, preferred_element_type=jnp.float32).astype(jnp.bfloat16)


def shared_mlp(tok_rows, shared_gate, shared_up, shared_down):
    gate_act = jnp.dot(tok_rows, shared_gate, preferred_element_type=jnp.float32)
    up_act = jnp.dot(tok_rows, shared_up, preferred_element_type=jnp.float32)
    hidden = (jax.nn.silu(gate_act) * up_act).astype(jnp.bfloat16)
    return jnp.dot(hidden, shared_down, preferred_element_type=jnp.float32).astype(jnp.bfloat16)


def solution(mesh):
    row_spec = P(('dp', 'ep'), None)
    full_spec = P(None, None)
    expert_spec = P('ep', None, None)

    def device_step(tok_rows, w_router, ids_loc, w_gate, w_up, w_down, shared_gate, shared_up, shared_down):
        tok_dev, top_k = ids_loc.shape
        num_exp = w_router.shape[1]
        capacity = capacity_of(tok_dev, top_k, num_exp)
        gate_vals = gate_values(tok_rows, w_router, ids_loc)
        slot_pos, buf_tok = dispatch_tables(ids_loc, num_exp, capacity)
        send_buf = jnp.take(tok_rows, buf_tok, axis=0, mode='fill', fill_value=0)
        recv_buf = lax.all_to_all(send_buf, 'ep', 0, 1, tiled=True)
        out_buf = expert_mlp(recv_buf, w_gate, w_up, w_down)
        back_buf = lax.all_to_all(out_buf, 'ep', 1, 0, tiled=True)
        picked_rows = jnp.take(back_buf.reshape(num_exp * capacity, -1), slot_pos, axis=0)
        routed = jnp.sum(gate_vals[:, :, None] * picked_rows.astype(jnp.float32), axis=1)
        shared_out = shared_mlp(tok_rows, shared_gate, shared_up, shared_down)
        return (shared_out.astype(jnp.float32) + routed).astype(jnp.bfloat16)

    return jax.shard_map(device_step, mesh=mesh, in_specs=(row_spec, full_spec, row_spec, expert_spec, expert_spec, expert_spec, full_spec, full_spec, full_spec), out_specs=row_spec, check_vma=False)
```

profile of v0, /device:TPU:81, one launch (start us, length us, event | category | flops | bytes accessed | tf_op | source)
XLA Modules:
  0.0 1604.6 jit_solution(2380812166664514490)
XLA Ops:
  2.4 42.9 %scatter_custom_fusion = s32[64]{0:T(128)S(1)} fusion(s32[6144]{0:T(1024)S(1)} %reshape.385, s32[6144]{0:T(1024)S(1)} %broadcast.397, s32[]{:T(128)} %constant.37.clone.1), kind=kCustom, calls=%fused_computation.110 | custom fusion | flops 6144 | bytes 260 | tf_op jit(solution)/shard_map/scatter-add | solution.py:24
  46.2 6.7 sort.17
  52.9 51.2 %gather_fusion.1 = s32[9216]{0:T(1024)S(1)} fusion(s32[6144]{0:T(1024)S(1)} %get-tuple-element.6, s32[9216]{0:T(1024)S(1)} %broadcast_clamp_fusion.1), kind=kCustom, calls=%fused_computation.1 | custom fusion | bytes 110592 | tf_op jit(solution)/shard_map/gather | solution.py:31
  104.7 71.6 %gather_fusion.2 = bf16[9216,2048]{1,0:T(8,128)(2,1)} fusion(bf16[1024,2048]{1,0:T(8,128)(2,1)} %param.9, s32[9216]{0:T(1024)S(1)} %broadcast_clamp_fusion), kind=kCustom, calls=%fused_computation.2 | custom fusion | bytes 75534336 | tf_op jit(solution)/shard_map/jit(_take)/gather | solution.py:61
  176.4 25.7 %broadcast_select_fusion = bf16[64,144,2048]{2,1,0:T(8,128)(2,1)} fusion(bf16[64,144,2048]{2,1,0:T(8,128)(2,1)} %bitcast.107, pred[64,144]{1,0:T(8,128)(4,1)S(1)} %compare_and_fusion), kind=kLoop, calls=%fused_computation.11 | loop fusion | flops 18874368 | bytes 75506688 | tf_op jit(solution)/shard_map/jit(_take)/select_n | solution.py:61
  202.1 422.7 %all_to_all.33 = bf16[64,144,2048]{2,1,0:T(8,128)(2,1)} all-to-all(bf16[64,144,2048]{2,1,0:T(8,128)(2,1)} %broadcast_select_fusion), channel_id=1, replica_groups=mesh['dp'=4,'ep'=8] {'ep'}, dimensions={0} | all-to-all | bytes 75497472 | tf_op jit(solution)/shard_map/all_to_all | solution.py:62
  624.8 25.5 %copy.45 = bf16[8,8,144,2048]{3,2,1,0:T(8,128)(2,1)} copy(bf16[8,8,144,2048]{3,2,0,1:T(8,128)(2,1)} %bitcast.108) | data formatting | bytes 75497472 | tf_op jit(solution)/shard_map/all_to_all | solution.py:62
  650.3 67.0 %fusion.19 = f32[8,1152,1408]{2,1,0:T(8,128)} fusion(bf16[8,1152,2048]{2,1,0:T(8,128)(2,1)} %bitcast.109, bf16[8,2048,1408]{2,1,0:T(8,128)(2,1)} %param.12), kind=kOutput, calls=%fused_computation.121 | convolution fusion | flops 53150220288 | bytes 135790592 | tf_op jit(solution)/shard_map/ecd,edf->ecf/dot_general | solution.py:37
  717.3 74.1 %fusion.clone.4 = bf16[8,1152,1408]{2,1,0:T(8,128)(2,1)} fusion(bf16[8,1152,2048]{2,1,0:T(8,128)(2,1)} %bitcast.110, bf16[8,2048,1408]{2,1,0:T(8,128)(2,1)} %param.13, f32[8,1152,1408]{2,1,0:T(8,128)} %fusion.19), kind=kOutput, calls=%fused_computation.9.clone.clone.clone.1 | convolution fusion | flops 53228077056 | bytes 161742848 | tf_op jit(solution)/shard_map/ecd,edf->ecf/dot_general | solution.py:38
  791.4 69.5 %convolution_convert_fusion = bf16[8,1152,2048]{2,1,0:T(8,128)(2,1)} fusion(bf16[8,1408,2048]{2,1,0:T(8,128)(2,1)} %param.14, bf16[8,1152,1408]{2,1,0:T(8,128)(2,1)} %fusion.clone.4), kind=kOutput, calls=%fused_computation.10 | convolution fusion | flops 53169094656 | bytes 109838336 | tf_op jit(solution)/shard_map/ecf,efd->ecd/dot_general | solution.py:40
  860.9 33.4 %copy.46 = bf16[8,1152,2048]{2,0,1:T(8,128)(2,1)} copy(bf16[8,1152,2048]{2,1,0:T(8,128)(2,1)} %convolution_convert_fusion) | data formatting | bytes 75497472 | tf_op jit(solution)/shard_map/convert_element_type | solution.py:40
  894.3 8.9 all-to-all-start.1
  903.3 34.3 %gather_fusion = s32[6144]{0:T(1024)S(1)} fusion(s32[6144]{0:T(1024)S(1)} %copy-done.5, s32[6144]{0:T(1024)S(1)} %get-tuple-element.66), kind=kCustom, calls=%fused_computation | custom fusion | bytes 73728 | tf_op jit(solution)/shard_map/gather | solution.py:23
  940.4 4.6 compare_select_fusion.4
  949.4 36.1 %select_subtract_fusion = s32[6144]{0:T(1024)S(1)} fusion(pred[6144]{0:T(1024)(128)(4,1)S(1)} %get-tuple-element.63, pred[6144]{0:T(1024)(128)(4,1)S(1)} %get-tuple-element.62, pred[6144]{0:T(1024)(128)(4,1)S(1)} %get-tuple-element.61, pred[6144]{0:T(1024)(128)(4,1)S(1)} %get-tuple-element.60, pred[6144]{0:T(1024)(128)(4,1)S(1)} %get-tuple-element.59, ...), kind=kLoop, calls=%fused_computation.101 | loop fusion | flops 368640 | bytes 424164 | tf_op jit(solution)/shard_map/sub | solution.py:27
  985.5 23.0 %scatter_custom_fusion.1 = s32[6144]{0:T(1024)S(1)} fusion(s32[6144]{0:T(1024)S(1)} %get-tuple-element.67, s32[6144]{0:T(1024)S(1)} %select_subtract_fusion, s32[]{:T(128)} %constant.37.clone.1), kind=kCustom, calls=%fused_computation.108 | custom fusion | bytes 24580 | tf_op jit(solution)/shard_map/scatter | solution.py:28
  1016.1 49.5 %gather_fusion.4 = f32[6144]{0:T(1024)S(1)} fusion(f32[1024,64]{0,1:T(8,128)S(1)} %fusion.18, s32[6144]{0:T(1024)S(1)} %reshape.377), kind=kCustom, calls=%fused_computation.4 | custom fusion | bytes 98304 | tf_op jit(solution)/shard_map/jit(take_along_axis)/gather | solution.py:14
  1066.7 18.7 %fusion.17 = f32[1024,2816]{1,0:T(8,128)} fusion(bf16[1024,2048]{1,0:T(8,128)(2,1)} %param.9, bf16[2048,2816]{1,0:T(8,128)(2,1)} %param.15), kind=kOutput, calls=%fused_computation.119 | convolution fusion | flops 11811160064 | bytes 27262976 | tf_op jit(solution)/shard_map/dot_general | solution.py:44
  1085.4 225.8 %all-to-all-done.1 = bf16[8,1152,2048]{2,0,1:T(8,128)(2,1)} async-done(((bf16[8,1152,2048]{2,0,1:T(8,128)(2,1)}), bf16[8,1152,2048]{2,0,1:T(8,128)(2,1)}, u32[]{:S(2)}, u32[]{:S(2)}) %all-to-all-start.1) | async-done | bytes 37748768 | tf_op jit(solution)/shard_map/all_to_all | solution.py:64
  1311.3 33.7 %copy.47 = bf16[8,8,144,2048]{3,2,0,1:T(8,128)(2,1)} copy(bf16[8,8,144,2048]{3,0,2,1:T(8,128)(2,1)} %bitcast.72) | data formatting | bytes 75497472 | tf_op jit(solution)/shard_map/all_to_all | solution.py:64
  1345.0 143.6 %gather_fusion.3 = bf16[6144,2048]{1,0:T(8,128)(2,1)} fusion(bf16[9216,2048]{1,0:T(8,128)(2,1)} %bitcast.106, s32[6144]{0:T(1024)S(1)} %broadcast_clamp_fusion.2), kind=kCustom, calls=%fused_computation.3 | custom fusion | bytes 50356224 | tf_op jit(solution)/shard_map/jit(_take)/gather | solution.py:65
  1488.6 39.5 %reshape.370 = bf16[1024,6,2048]{2,1,0:T(8,128)(2,1)} reshape(bf16[6144,2048]{1,0:T(8,128)(2,1)} %gather_fusion.3) | data formatting | bytes 50331648 | tf_op jit(solution)/shard_map/jit(_take)/gather | solution.py:65
  1528.1 39.7 %multiply_reduce_fusion = f32[1024,2048]{1,0:T(8,128)} fusion(bf16[1024,6,2048]{2,1,0:T(8,128)(2,1)} %reshape.370, f32[1024,6]{1,0:T(8,128)S(1)} %copy.37, pred[1024,6]{1,0:T(8,128)(4,1)S(1)} %copy-done.10), kind=kLoop, calls=%fused_computation.8 | loop fusion | flops 48234496 | bytes 33585152 | tf_op jit(solution)/shard_map/reduce_sum | solution.py:66
  1567.8 36.3 %add_convert_fusion = bf16[1024,2048]{1,0:T(8,128)(2,1)} fusion(f32[1024,2048]{1,0:T(8,128)} %multiply_reduce_fusion, bf16[2816,2048]{1,0:T(8,128)(2,1)} %param.17, f32[1024,2816]{1,0:T(8,128)} %fusion.17, bf16[1024,2048]{1,0:T(8,128)(2,1)} %param.9, bf16[2048,2816]{1,0:T(8,128)(2,1)} %param.16), kind=kOutput, calls=%fused_computation.13 | convolution fusion | flops 23648010240 | bytes 51380224 | tf_op jit(solution)/shard_map/dot_general | solution.py:47
  (74 shorter events, 19.7 us)
Async XLA Ops:
  0.0 1012.5 %copy-start = (bf16[2048,64]{0,1:T(8,128)(2,1)S(1)}, bf16[2048,64]{0,1:T(8,128)(2,1)}, u32[]{:S(2)}) copy-start(bf16[2048,64]{0,1:T(8,128)(2,1)} %param.10) | copy-start | bytes 786436
  45.6 0.6 copy-start.6
  45.9 58.1 %copy-start.4 = (s32[6144]{0:T(1024)}, s32[6144]{0:T(1024)S(1)}, u32[]{:S(2)}) copy-start(s32[6144]{0:T(1024)S(1)} %reshape.268) | copy-start | bytes 73732
  52.9 51.2 %copy-start.2 = (s32[6144]{0:T(1024)}, s32[6144]{0:T(1024)S(1)}, u32[]{:S(2)}) copy-start(s32[6144]{0:T(1024)S(1)} %get-tuple-element.6) | copy-start | bytes 73732
  894.3 8.9 copy-start.3
  894.3 8.9 copy-start.5
  894.3 416.9 %all-to-all-start.1 = ((bf16[8,1152,2048]{2,0,1:T(8,128)(2,1)}), bf16[8,1152,2048]{2,0,1:T(8,128)(2,1)}, u32[]{:S(2)}, u32[]{:S(2)}) async-start(bf16[8,1152,2048]{2,0,1:T(8,128)(2,1)} %copy.46), calls=%async_computation.1 | async-start | bytes 75497472 | tf_op jit(solution)/shard_map/all_to_all | solution.py:64
  903.2 34.3 %copy-start.7 = (s32[64]{0:T(128)S(1)}, s32[64]{0:T(128)}, u32[]{:S(2)}) copy-start(s32[64]{0:T(128)} %copy-done.6) | copy-start | bytes 772
  903.2 108.7 %copy-start.8 = (s32[1024,6]{0,1:T(8,128)S(1)}, s32[1024,6]{0,1:T(8,128)}, u32[]{:S(2)}) copy-start(s32[1024,6]{0,1:T(8,128)} %param.11) | copy-start | bytes 73732
  1016.1 50.2 %copy-start.9 = (s32[1024,6]{0,1:T(8,128)S(1)}, s32[1024,6]{0,1:T(8,128)}, u32[]{:S(2)}) copy-start(s32[1024,6]{0,1:T(8,128)} %param.11) | copy-start | bytes 73732
  1016.1 50.6 %copy-start.11 = (s32[6144]{0:T(1024)S(1)}, s32[6144]{0:T(1024)}, u32[]{:S(2)}) copy-start(s32[6144]{0:T(1024)} %reshape.371) | copy-start | bytes 73732
  1488.6 39.5 %copy-start.10 = (pred[1024,6]{1,0:T(8,128)(4,1)S(1)}, pred[1024,6]{1,0:T(8,128)(4,1)}, u32[]{:S(2)}) copy-start(pred[1024,6]{1,0:T(8,128)(4,1)} %copy.44) | copy-start | bytes 18436
  1567.8 36.3 %copy-start.1 = (bf16[2048,64]{0,1:T(8,128)(2,1)S(1)}, bf16[2048,64]{0,1:T(8,128)(2,1)}, u32[]{:S(2)}) copy-start(bf16[2048,64]{0,1:T(8,128)(2,1)} %param.10) | copy-start | bytes 786436
where the time goes:
time: 1620 us; the launch traced here: 1600 us
  local copies, waits for them, and re-layouts  516 us (32%)
  blocking collectives  423 us (26%)
  matrix products  269 us (17%)
  waiting for transfers between devices  226 us (14%)
  other arithmetic  162 us (10%)
    all_to_all x1, blocking collectives, device_step(): recv_buf = lax.all_to_all(send_buf, 'ep', 0, 1, tiled=True)  423 us
    all_to_all x1, waiting for transfers between devices, device_step(): back_buf = lax.all_to_all(out_buf, 'ep', 1, 0, tiled=True)  226 us
    gather x2, local copies, waits for them, and re-layouts, device_step(): jnp.take(back_buf.reshape(num_exp * capacity, -1), slot_pos, axis=0)  183 us
    dot_general x1, matrix products, expert_mlp(): jnp.einsum('ecd,edf->ecf', rows_in, w_up, preferred_element_type=jnp.floa...  74.1 us
    gather x1, local copies, waits for them, and re-layouts, device_step(): send_buf = jnp.take(tok_rows, buf_tok, axis=0, mode='fill', fill_value=0)  71.6 us
    dot_general x1, matrix products, expert_mlp(): jnp.einsum('ecf,efd->ecd', hidden, w_down, preferred_element_type=jnp.flo...  69.5 us
    dot_general x1, matrix products, expert_mlp(): jnp.einsum('ecd,edf->ecf', rows_in, w_gate, preferred_element_type=jnp.fl...  67 us
    gather x1, local copies, waits for them, and re-layouts, dispatch_tables(): pair_id = sort_order[src_pos]  51.2 us
  transfers between devices with their start and end apart: 1, of which 1 were waited for; matrix products, arithmetic and copies ran while one was open for 11% of the time, Pallas kernels for 0%

commit v1 on v0

v1 whole, which is shorter than its diff:
```python
import functools

import jax
import jax.numpy as jnp
from jax import lax
from jax.experimental import pallas as pl
from jax.experimental.pallas import tpu as pltpu
from jax.sharding import PartitionSpec as P


LANES = 128
BLOCK_ROWS = 256
SLAB = 24
CHUNK = 256


def capacity_of(tok_dev, top_k, num_exp):
    base_load = tok_dev * top_k // num_exp
    return base_load + base_load // 2 + min(tok_dev * top_k % num_exp, 1)


def experts_kernel(table_cap, num_after, count_s, tok_s, gate_s, seg_a, seg_b, seg_c, seg_d, w_gate, w_up, w_down, *refs):
    (out_mine, out_other, tok_v, acc, buf_g, buf_u, buf_d, slab_v, rows_v, hid_v,
     sem_tok, sem_g, sem_u, sem_d, sem_out) = refs[num_after:]
    num_loc, model_dim, ff_dim = w_gate.shape
    half = seg_a.shape[0]
    pieces = seg_a.shape[1]
    num_rows = 4 * half

    def load_gu(exp):
        slot = lax.rem(exp, 2)
        return (pltpu.make_async_copy(w_gate.at[exp], buf_g.at[slot], sem_g.at[slot]),
                pltpu.make_async_copy(w_up.at[exp], buf_u.at[slot], sem_u.at[slot]))

    def load_d(exp):
        return pltpu.make_async_copy(w_down.at[exp], buf_d, sem_d)

    seg_copies = [pltpu.make_async_copy(seg, tok_v.at[pl.ds(half * idx, half)], sem_tok.at[idx])
                  for idx, seg in enumerate((seg_a, seg_b, seg_c, seg_d))]
    for copy in seg_copies:
        copy.start()
    for copy in load_gu(0):
        copy.start()
    load_d(0).start()

    def clear(idx, carry):
        acc[pl.ds(idx * 8, 8)] = jnp.zeros((8, pieces, LANES), jnp.float32)
        return carry

    lax.fori_loop(0, num_rows // 8, clear, 0)
    tok_v[num_rows] = jnp.zeros((pieces, LANES), jnp.bfloat16)
    acc[num_rows] = jnp.zeros((pieces, LANES), jnp.float32)
    for copy in seg_copies:
        copy.wait()

    def expert(exp, carry):
        slot = lax.rem(exp, 2)

        @pl.when(exp + 1 < num_loc)
        def _():
            for copy in load_gu(exp + 1):
                copy.start()

        count = count_s[exp]
        num_blocks = jnp.maximum((count + BLOCK_ROWS - 1) // BLOCK_ROWS, 1)

        def block(blk, carry):
            base = exp * table_cap + blk * BLOCK_ROWS
            groups = (jnp.minimum(count - blk * BLOCK_ROWS, BLOCK_ROWS) + 7) // 8

            def fetch(grp, carry):
                for lane in range(8):
                    row = grp * 8 + lane
                    slab_v[pl.ds(pl.multiple_of(row * SLAB, 8), pieces), :] = tok_v[tok_s[base + row]].astype(jnp.float32)
                return carry

            lax.fori_loop(0, groups, fetch, 0)
            for col in range(pieces):
                rows_v[:, col * LANES:(col + 1) * LANES] = slab_v[pl.ds(col, BLOCK_ROWS, stride=SLAB), :].astype(jnp.bfloat16)

            @pl.when(blk == 0)
            def _():
                for copy in load_gu(exp):
                    copy.wait()

            for start in range(0, ff_dim, CHUNK):
                width = min(CHUNK, ff_dim - start)
                cols = slice(start, start + width)
                gate_act = jnp.dot(rows_v[...], buf_g[slot, :, cols], preferred_element_type=jnp.float32)
                up_act = jnp.dot(rows_v[...], buf_u[slot, :, cols], preferred_element_type=jnp.float32)
                hid_v[:, cols] = (jax.nn.silu(gate_act) * up_act).astype(jnp.bfloat16)

            @pl.when(blk == 0)
            def _():
                load_d(exp).wait()

            for start in range(0, model_dim, CHUNK):
                out_rows = jnp.dot(hid_v[...], buf_d[:, start:start + CHUNK], preferred_element_type=jnp.float32)
                out_rows = out_rows.astype(jnp.bfloat16).astype(jnp.float32)
                for off in range(0, CHUNK, LANES):
                    slab_v[pl.ds((start + off) // LANES, BLOCK_ROWS, stride=SLAB), :] = out_rows[:, off:off + LANES]

            @pl.when((blk == num_blocks - 1) & (exp + 1 < num_loc))
            def _():
                load_d(exp + 1).start()

            def combine(grp, carry):
                toks, sums = [], []
                for lane in range(8):
                    row = grp * 8 + lane
                    tok = tok_s[base + row]
                    piece = slab_v[pl.ds(pl.multiple_of(row * SLAB, 8), pieces), :]
                    toks.append(tok)
                    sums.append(acc[tok] + gate_s[base + row] * piece)
                for tok, val in zip(toks, sums):
                    acc[tok] = val
                return carry

            lax.fori_loop(0, groups, combine, 0)
            return carry

        lax.fori_loop(0, num_blocks, block, 0)
        return carry

    lax.fori_loop(0, num_loc, expert, 0)
    outs = [pltpu.make_async_copy(acc.at[pl.ds(2 * half * idx, 2 * half)], out, sem_out.at[idx])
            for idx, out in enumerate((out_mine, out_other))]
    for copy in outs:
        copy.start()
    for copy in outs:
        copy.wait()


def expert_pass(counts, toks, gates, segs, w_gate, w_up, w_down, table_cap, after):
    num_loc, model_dim, ff_dim = w_gate.shape
    half, pieces, _ = segs[0].shape
    num_rows = 4 * half
    out_type = jax.ShapeDtypeStruct((2 * half, pieces, LANES), jnp.float32)
    any_spec = pl.BlockSpec(memory_space=pl.ANY)
    smem_spec = pl.BlockSpec(memory_space=pltpu.SMEM)
    avg_rows = num_rows * 6 // 8
    return pl.pallas_call(
        functools.partial(experts_kernel, table_cap, len(after)),
        out_shape=(out_type, out_type),
        in_specs=[smem_spec] * 3 + [any_spec] * (7 + len(after)),
        out_specs=(any_spec, any_spec),
        scratch_shapes=[
            pltpu.VMEM((num_rows + 8, pieces, LANES), jnp.bfloat16),
            pltpu.VMEM((num_rows + 8, pieces, LANES), jnp.float32),
            pltpu.VMEM((2, model_dim, ff_dim), jnp.bfloat16),
            pltpu.VMEM((2, model_dim, ff_dim), jnp.bfloat16),
            pltpu.VMEM((ff_dim, model_dim), jnp.bfloat16),
            pltpu.VMEM((BLOCK_ROWS * SLAB, LANES), jnp.float32),
            pltpu.VMEM((BLOCK_ROWS, model_dim), jnp.bfloat16),
            pltpu.VMEM((BLOCK_ROWS, ff_dim), jnp.bfloat16),
            pltpu.SemaphoreType.DMA((4,)),
            pltpu.SemaphoreType.DMA((2,)),
            pltpu.SemaphoreType.DMA((2,)),
            pltpu.SemaphoreType.DMA,
            pltpu.SemaphoreType.DMA((2,)),
        ],
        compiler_params=pltpu.CompilerParams(vmem_limit_bytes=63 * 1024 * 1024),
        cost_estimate=pl.CostEstimate(flops=6 * avg_rows * model_dim * ff_dim * 3 // 2, transcendentals=0,
                                      bytes_accessed=3 * num_loc * model_dim * ff_dim * 2),
        name='experts',
    )(counts, toks, gates, *segs, w_gate, w_up, w_down, *after)


def finish_kernel(blocks_half, shared_ref, mine_ref, other_ref, near_a, near_b, far_a, far_b, out_ref, sum_v):
    rows = shared_ref.shape[0]
    pieces = mine_ref.shape[1]
    idx = pl.program_id(0)
    flat = (rows * pieces, LANES)

    def gather_sum(near, far):
        total = (mine_ref[...] + other_ref[...]) + (near[...] + far[...])
        sum_v[...] = total.reshape(flat)

    pl.when(idx < blocks_half)(lambda: gather_sum(near_a, far_a))
    pl.when(idx >= blocks_half)(lambda: gather_sum(near_b, far_b))
    for col in range(pieces):
        cols = slice(col * LANES, (col + 1) * LANES)
        out_ref[:, cols] = (shared_ref[:, cols].astype(jnp.float32) + sum_v[pl.ds(col, rows, stride=pieces), :]).astype(jnp.bfloat16)


def finish(shared_out, mine, other, near_a, near_b, far_a, far_b):
    tok_dev, model_dim = shared_out.shape
    pieces = mine.shape[1]
    rows = 128
    blocks_half = tok_dev // rows // 2
    full = lambda idx: (idx, 0, 0)
    first = lambda idx: (jnp.minimum(idx, blocks_half - 1), 0, 0)
    second = lambda idx: (jnp.maximum(idx - blocks_half, 0), 0, 0)
    slab = (rows, pieces, LANES)
    return pl.pallas_call(
        functools.partial(finish_kernel, blocks_half),
        out_shape=jax.ShapeDtypeStruct((tok_dev, model_dim), jnp.bfloat16),
        grid=(tok_dev // rows,),
        in_specs=[pl.BlockSpec((rows, model_dim), lambda idx: (idx, 0)), pl.BlockSpec(slab, full), pl.BlockSpec(slab, full),
                  pl.BlockSpec(slab, first), pl.BlockSpec(slab, second), pl.BlockSpec(slab, first), pl.BlockSpec(slab, second)],
        out_specs=pl.BlockSpec((rows, model_dim), lambda idx: (idx, 0)),
        scratch_shapes=[pltpu.VMEM((rows * pieces, LANES), jnp.float32)],
        compiler_params=pltpu.CompilerParams(vmem_limit_bytes=48 * 1024 * 1024),
        cost_estimate=pl.CostEstimate(flops=tok_dev * model_dim * 8, transcendentals=0, bytes_accessed=tok_dev * model_dim * 20),
        name='finish',
    )(shared_out, mine, other, near_a, near_b, far_a, far_b)


def shared_hidden(tok_rows, shared_gate, shared_up):
    gate_act = jnp.dot(tok_rows, shared_gate, preferred_element_type=jnp.float32)
    up_act = jnp.dot(tok_rows, shared_up, preferred_element_type=jnp.float32)
    return (jax.nn.silu(gate_act) * up_act).astype(jnp.bfloat16)


def routing_exchange(tok_rows, w_router, ids_loc):
    top_k = ids_loc.shape[1]
    num_exp = w_router.shape[1]
    logits = lax.dot_general(w_router, tok_rows, (((0,), (1,)), ((), ())), preferred_element_type=jnp.float32)
    ids = ids_loc.T
    exp_range = jnp.arange(num_exp, dtype=jnp.int32)[:, None]
    picked = jnp.stack([jnp.sum(jnp.where(ids[k][None, :] == exp_range, logits, 0.0), axis=0) for k in range(top_k)])
    gates = jax.nn.softmax(picked, axis=0)
    packed = jnp.concatenate([ids.astype(jnp.float32), gates], axis=0)
    return lax.all_gather(packed, 'ep')


def routing_tables(everyone, num_exp, group, table_cap):
    top_k, tok_dev = everyone.shape[1] // 2, everyone.shape[2]
    num_loc = num_exp // group
    half = tok_dev // 2
    me = lax.axis_index('ep')
    chip, core = me // 2, me % 2
    chips = group // 2
    order = [((chip + off) % chips) * 2 + side for off in range(chips) for side in (core, 1 - core)]
    rolled = jnp.stack([lax.dynamic_index_in_dim(everyone, src, 0, keepdims=False) for src in order])
    mine = (me * num_loc + jnp.arange(num_loc, dtype=jnp.int32)).astype(jnp.float32)[None, :, None]
    named = jnp.zeros((group, num_loc, tok_dev), jnp.bool_)
    gate = jnp.zeros((group, num_loc, tok_dev), jnp.float32)
    for k in range(top_k):
        hit = rolled[:, k][:, None, :] == mine
        named = named | hit
        gate = gate + jnp.where(hit, rolled[:, top_k + k][:, None, :], 0.0)
    segs = [[(6, 0), (2, 1), (7, 0), (3, 1)],
            [(4, 0), (4, 1), (5, 0), (5, 1)],
            [(6, 1), (2, 0), (7, 1), (3, 0)],
            [(0, 0), (0, 1), (1, 0), (1, 1)]]

    def arrange(table):
        return jnp.stack([jnp.concatenate([table[src, :, side * half:(side + 1) * half] for src, side in seg], axis=1) for seg in segs])

    named, gate = arrange(named), arrange(gate)
    num_rows = 2 * tok_dev
    key = jnp.where(named, jnp.arange(num_rows, dtype=jnp.int32), num_rows)
    counts = jnp.sum(named.astype(jnp.int32), axis=2)
    key, gate = lax.sort((key, gate), dimension=2, num_keys=1, is_stable=False)
    flat = (len(segs), num_loc * table_cap)
    return counts, key[:, :, :table_cap].reshape(flat), gate[:, :, :table_cap].reshape(flat)


def solution(mesh):
    group = mesh.shape['ep']
    row_spec = P(('dp', 'ep'), None)
    full_spec = P(None, None)
    expert_spec = P('ep', None, None)
    forward = [(dev, (dev + 2) % group) for dev in range(group)]
    backward = [(dev, (dev - 2) % group) for dev in range(group)]
    across = [(dev, dev ^ 1) for dev in range(group)]

    def send(array, route):
        return lax.ppermute(array, 'ep', route)

    def device_step(tok_rows, w_router, ids_loc, w_gate, w_up, w_down, shared_gate, shared_up, shared_down):
        tok_dev, model_dim = tok_rows.shape
        top_k = ids_loc.shape[1]
        num_exp = w_router.shape[1]
        half = tok_dev // 2
        pieces = model_dim // LANES
        worst = 4 * capacity_of(tok_dev, top_k, num_exp)
        table_cap = -(-worst // BLOCK_ROWS) * BLOCK_ROWS

        slabs = tok_rows.reshape(tok_dev, pieces, LANES)
        own_a, own_b = slabs[:half], slabs[half:]
        everyone = routing_exchange(tok_rows, w_router, ids_loc)
        own_a, own_b, everyone = lax.optimization_barrier((own_a, own_b, everyone))
        left_a = send(own_a, forward)
        right_b = send(own_b, backward)
        pair_a, pair_b = send(own_a, across), send(own_b, across)

        counts, toks, gates = routing_tables(everyone, num_exp, group, table_cap)

        def run(idx, segs, after):
            mine, other = expert_pass(counts[idx], toks[idx], gates[idx], segs, w_gate, w_up, w_down, table_cap, after)
            return mine, send(other, across)

        hidden = shared_hidden(tok_rows, shared_gate, shared_up)
        far_a, far_b = send(left_a, forward), send(right_b, backward)
        left_b, right_a = send(own_b, forward), send(own_a, backward)

        segs = [left_a, right_b, send(left_a, across), send(right_b, across)]
        mine, other = run(0, segs, [hidden])
        shared_out = jnp.dot(hidden, shared_down, preferred_element_type=jnp.float32).astype(jnp.bfloat16)
        to_left, to_right = mine[:half] + other[:half], mine[half:] + other[half:]
        near_a, near_b = send(to_left, backward), send(to_right, forward)

        segs = [far_a, far_b, send(far_a, across), send(far_b, across)]
        mine, other = run(1, segs, [to_left, to_right, shared_out])
        to_right, to_left = mine[:half] + other[:half], mine[half:] + other[half:]
        via_a, via_b = send(to_right, forward), send(to_left, backward)

        segs = [left_b, right_a, send(left_b, across), send(right_a, across)]
        mine, other = run(2, segs, [to_left, to_right])
        to_left, to_right = mine[:half] + other[:half] + via_b, mine[half:] + other[half:] + via_a
        last_b, last_a = send(to_left, backward), send(to_right, forward)

        mine, other = run(3, [own_a, own_b, pair_a, pair_b], [to_left, to_right])
        return finish(shared_out, mine, other, near_a, near_b, last_a, last_b)

    return jax.shard_map(device_step, mesh=mesh, in_specs=(row_spec, full_spec, row_spec, expert_spec, expert_spec, expert_spec, full_spec, full_spec, full_spec), out_specs=row_spec, check_vma=False)
```

time: 1620 us -> 905 us (0.56)
  local copies, waits for them, and re-layouts: 516 us -> 30.1 us
  blocking collectives: 423 us -> 15.1 us
  Pallas kernels: 0 us -> 324 us
  matrix products: 269 us -> 59 us
  waiting for transfers between devices: 226 us -> 383 us
  other arithmetic: 162 us -> 35.9 us
  starting transfers between devices: 8.87 us -> 38.2 us
    all_to_all x1 -> x0, blocking collectives: 423 us -> none  [device_step(): recv_buf = lax.all_to_all(send_buf, 'ep', 0, 1, tiled=True)]
    gather x14 -> x0, local copies, waits for them, and re-layouts: 394 us -> none  [the longest x2 183 us: device_step(): jnp.take(back_buf.reshape(num_exp * capacity, -1), slot_pos, axis=0)]
    ppermute x0 -> x24, waiting for transfers between devices: none -> 383 us  [send(): return lax.ppermute(array, 'ep', route)]
    pallas_call x0 -> x5, Pallas kernels: none -> 324 us  [the longest x4 309 us: expert_pass(): pl.pallas_call(functools.partial(experts_kernel, table_cap, len(after)),...]
    all_to_all x1 -> x0, waiting for transfers between devices: 226 us -> none  [device_step(): back_buf = lax.all_to_all(out_buf, 'ep', 1, 0, tiled=True)]
    dot_general x6 -> x4, matrix products: 269 us -> 59 us  [the longest x1 20.2 us: shared_hidden(): jnp.dot(tok_rows, shared_gate, preferred_element_type=jnp.float32)]
    all_to_all x2 -> x0, local copies, waits for them, and re-layouts: 59.2 us -> none  [the longest x1 33.7 us: device_step(): back_buf = lax.all_to_all(out_buf, 'ep', 1, 0, tiled=True)]
    scatter-add x1 -> x0, other arithmetic: 42.9 us -> none  [dispatch_tables(): counts = jnp.bincount(flat_ids, length=num_exp)]
  transfers between devices with their start and end apart: 1 -> 24, of which waited for: 1 -> 8; matrix products, arithmetic and copies ran while one was open for 11% -> 11% of each run, Pallas kernels for 0% -> 0%
where the time goes in v1:
time: 905 us; the launch traced here: 900 us
  waiting for transfers between devices  383 us (42%)
  Pallas kernels  324 us (36%)
  matrix products  59 us (7%)
  starting transfers between devices  38.2 us (4%)
  other arithmetic  35.9 us (4%)
  local copies, waits for them, and re-layouts  30.1 us (3%)
  blocking collectives  15.1 us (2%)
  between operations  14.1 us (2%)
    ppermute x24, waiting for transfers between devices, send(): return lax.ppermute(array, 'ep', route)  383 us
    pallas_call x4, Pallas kernels, expert_pass(): pl.pallas_call(functools.partial(experts_kernel, table_cap, len(after)),...  309 us
    ppermute x24, starting transfers between devices, send(): return lax.ppermute(array, 'ep', route)  38.2 us
    unnamed x47, local copies, waits for them, and re-layouts  20.5 us
    dot_general x1, matrix products, shared_hidden(): jnp.dot(tok_rows, shared_gate, preferred_element_type=jnp.float32)  20.2 us
    dot_general x1, matrix products, shared_hidden(): up_act = jnp.dot(tok_rows, shared_up, preferred_element_type=jnp.float32)  19.1 us
  transfers between devices with their start and end apart: 24, of which 8 were waited for; matrix products, arithmetic and copies ran while one was open for 11% of the time, Pallas kernels for 0%

profile of v1, /device:TPU:81, one launch (start us, length us, event | category | flops | bytes accessed | tf_op | source)
XLA Modules:
  0.0 899.8 jit_solution(2299429479739149515)
XLA Ops:
  8.4 5.0 slice_bitcast_fusion
  15.2 15.1 %all-gather.1 = f32[8,12,1024]{2,1,0:T(8,128)S(1)} all-gather(f32[1,12,1024]{2,1,0:T(8,128)S(1)} %maximum_bitcast_fusion), channel_id=2, replica_groups=mesh['dp'=4,'ep'=8] {'ep'}, dimensions={0}, use_global_device_ids=true | all-gather | bytes 442368 | tf_op jit(solution)/shard_map/all_gather | solution.py:224
  32.5 4.3 copy.23
  42.3 20.2 %fusion.13 = f32[1024,2816]{1,0:T(8,128)} fusion(bf16[1024,2048]{1,0:T(8,128)(2,1)} %param.9, bf16[2048,2816]{1,0:T(8,128)(2,1)} %param.15), kind=kOutput, calls=%fused_computation.119 | convolution fusion | flops 11811160064 | bytes 27262976 | tf_op jit(solution)/shard_map/dot_general | solution.py:210
  62.5 22.6 %collective-permute-done.6.seg_a = bf16[512,16,128]{2,1,0:T(8,128)(2,1)} collective-permute-done((bf16[512,16,128]{2,1,0:T(8,128)(2,1)S(1)}, bf16[512,16,128]{2,1,0:T(8,128)(2,1)}, u32[]{:S(2)}, u32[]{:S(2)}) %collective-permute-start.6) | collective-permute-done | bytes 2097184 | tf_op jit(solution)/shard_map/ppermute | solution.py:270
  86.2 19.1 %multiply_convert_fusion.refs_0_ = bf16[1024,2816]{1,0:T(8,128)(2,1)} fusion(f32[1024,2816]{1,0:T(8,128)} %fusion.13, bf16[1024,2048]{1,0:T(8,128)(2,1)S(1)} %copy-done.10, bf16[2048,2816]{1,0:T(8,128)(2,1)} %param.16), kind=kOutput, calls=%fused_computation | convolution fusion | flops 11828461568 | bytes 33030144 | tf_op jit(solution)/shard_map/dot_general | solution.py:211
  109.9 72.8 %experts.4 = (f32[1024,16,128]{2,1,0:T(8,128)}, f32[1024,16,128]{2,1,0:T(8,128)}) custom-call(s32[8]{0:T(128)} %get-tuple-element.106.count_s, s32[6144]{0:T(1024)} %squeeze.183.tok_s, f32[6144]{0:T(1024)} %squeeze.184.gate_s, bf16[512,16,128]{2,1,0:T(8,128)(2,1)} %collective-permute-done.6.seg_a, bf16[512,16,128]{2,1,0:T(8,128)(2,1)} %collective-permute-done.8.seg_b, ...), custom_call_target="tpu_custom_call" | custom-call | flops 39862665216 | bytes 138412032 | tf_op jit(solution)/shard_map/experts/pallas_call | solution.py:142
  184.0 5.0 collective-permute-start.7
  190.5 45.7 %collective-permute-done.7.seg_a = bf16[512,16,128]{2,1,0:T(8,128)(2,1)S(1)} collective-permute-done((bf16[512,16,128]{2,1,0:T(8,128)(2,1)}, bf16[512,16,128]{2,1,0:T(8,128)(2,1)S(1)}, u32[]{:S(2)}, u32[]{:S(2)}) %collective-permute-start.7) | collective-permute-done | bytes 2097184 | tf_op jit(solution)/shard_map/ppermute | solution.py:270
  237.7 18.0 %convolution_convert_fusion.refs_2_.shared_ref = bf16[1024,2048]{1,0:T(8,128)(2,1)} fusion(bf16[1024,2816]{1,0:T(8,128)(2,1)} %multiply_convert_fusion.refs_0_, bf16[2816,2048]{1,0:T(8,128)(2,1)} %param.17), kind=kOutput, calls=%fused_computation.9 | convolution fusion | flops 11813257216 | bytes 21495808 | tf_op jit(solution)/shard_map/dot_general | solution.py:301
  256.9 10.2 %slice_add_fusion.4 = (f32[512,16,128]{2,1,0:T(8,128)}, f32[512,16,128]{2,1,0:T(8,128)}) fusion(f32[1024,16,128]{2,1,0:T(8,128)} %collective-permute-done.14, f32[1024,16,128]{2,1,0:T(8,128)} %get-tuple-element.23), kind=kLoop, calls=%fused_computation.7 | loop fusion | flops 2097152 | bytes 25165824 | tf_op jit(solution)/shard_map/add | solution.py:302
  267.1 72.7 %experts.5 = (f32[1024,16,128]{2,1,0:T(8,128)}, f32[1024,16,128]{2,1,0:T(8,128)}) custom-call(s32[8]{0:T(128)} %get-tuple-element.107.count_s, s32[6144]{0:T(1024)} %squeeze.180.tok_s, f32[6144]{0:T(1024)} %squeeze.181.gate_s, bf16[512,16,128]{2,1,0:T(8,128)(2,1)} %copy-done.11, bf16[512,16,128]{2,1,0:T(8,128)(2,1)} %collective-permute-done.9.seg_b, ...), custom_call_target="tpu_custom_call" | custom-call | flops 39862665216 | bytes 138412032 | tf_op jit(solution)/shard_map/experts/pallas_call | solution.py:142
  339.8 12.6 %collective-permute-start.15 = (f32[1024,16,128]{2,1,0:T(8,128)}, f32[1024,16,128]{2,1,0:T(8,128)}, u32[]{:S(2)}, u32[]{:S(2)}) collective-permute-start(f32[1024,16,128]{2,1,0:T(8,128)} %get-tuple-element.26), channel_id=1, source_target_pairs={{0,1},{1,0},{2,3},{3,2},{4,5},{5,4},{6,7},{7,6},{8,9},{9,8},{10,11... | collective-permute-start | bytes 25165832 | tf_op jit(solution)/shard_map/ppermute | solution.py:270
  352.4 2.7 collective-permute-start.3
  355.0 45.8 %collective-permute-done.2.seg_a = bf16[512,16,128]{2,1,0:T(8,128)(2,1)S(1)} collective-permute-done((bf16[512,16,128]{2,1,0:T(8,128)(2,1)}, bf16[512,16,128]{2,1,0:T(8,128)(2,1)S(1)}, u32[]{:S(2)}, u32[]{:S(2)}) %collective-permute-start.2) | collective-permute-done | bytes 2097184 | tf_op jit(solution)/shard_map/ppermute | solution.py:270
  403.1 10.2 %slice_add_fusion.2 = (f32[512,16,128]{2,1,0:T(8,128)}, f32[512,16,128]{2,1,0:T(8,128)}) fusion(f32[1024,16,128]{2,1,0:T(8,128)} %collective-permute-done.15, f32[1024,16,128]{2,1,0:T(8,128)} %get-tuple-element.25), kind=kLoop, calls=%fused_computation.5 | loop fusion | flops 2097152 | bytes 25165824 | tf_op jit(solution)/shard_map/add | solution.py:307
  413.3 78.6 %experts.6 = (f32[1024,16,128]{2,1,0:T(8,128)}, f32[1024,16,128]{2,1,0:T(8,128)}) custom-call(s32[8]{0:T(128)} %get-tuple-element.105.count_s, s32[6144]{0:T(1024)} %squeeze.177.tok_s, f32[6144]{0:T(1024)} %squeeze.178.gate_s, bf16[512,16,128]{2,1,0:T(8,128)(2,1)} %copy-done.12, bf16[512,16,128]{2,1,0:T(8,128)(2,1)} %collective-permute-done.3.seg_b, ...), custom_call_target="tpu_custom_call" | custom-call | flops 39862665216 | bytes 138412032 | tf_op jit(solution)/shard_map/experts/pallas_call | solution.py:142
  496.5 89.0 %collective-permute-done.17 = f32[512,16,128]{2,1,0:T(8,128)} collective-permute-done((f32[512,16,128]{2,1,0:T(8,128)}, f32[512,16,128]{2,1,0:T(8,128)}, u32[]{:S(2)}, u32[]{:S(2)}) %collective-permute-start.17) | collective-permute-done | bytes 4194336 | tf_op jit(solution)/shard_map/ppermute | solution.py:270
  586.6 12.6 %fusion = (f32[512,16,128]{2,1,0:T(8,128)}, f32[512,16,128]{2,1,0:T(8,128)}) fusion(f32[512,16,128]{2,1,0:T(8,128)} %collective-permute-done.18, f32[1024,16,128]{2,1,0:T(8,128)} %collective-permute-done.16, f32[1024,16,128]{2,1,0:T(8,128)} %get-tuple-element.27, f32[512,16,128]{2,1,0:T(8,128)} %collective-permute-done.17), kind=kLoop, calls=%fused_computation.2 | loop fusion | flops 4194304 | bytes 33554432 | tf_op jit(solution)/shard_map/add | solution.py:312
  599.2 84.5 %experts.7 = (f32[1024,16,128]{2,1,0:T(8,128)}, f32[1024,16,128]{2,1,0:T(8,128)}) custom-call(s32[8]{0:T(128)} %get-tuple-element.108.count_s, s32[6144]{0:T(1024)} %squeeze.174.tok_s, f32[6144]{0:T(1024)} %squeeze.175.gate_s, bf16[512,16,128]{2,1,0:T(8,128)(2,1)} %bitcast.145, bf16[512,16,128]{2,1,0:T(8,128)(2,1)} %bitcast.73.seg_b, ...), custom_call_target="tpu_custom_call" | custom-call | flops 39862665216 | bytes 138412032 | tf_op jit(solution)/shard_map/experts/pallas_call | solution.py:142
  689.3 88.1 %collective-permute-done.20.near_a = f32[512,16,128]{2,1,0:T(8,128)S(1)} collective-permute-done((f32[512,16,128]{2,1,0:T(8,128)}, f32[512,16,128]{2,1,0:T(8,128)S(1)}, u32[]{:S(2)}, u32[]{:S(2)}) %collective-permute-start.20) | collective-permute-done | bytes 4194336 | tf_op jit(solution)/shard_map/ppermute | solution.py:270
  778.5 89.9 %collective-permute-done.22.far_a = f32[512,16,128]{2,1,0:T(8,128)S(1)} collective-permute-done((f32[512,16,128]{2,1,0:T(8,128)}, f32[512,16,128]{2,1,0:T(8,128)S(1)}, u32[]{:S(2)}, u32[]{:S(2)}) %collective-permute-start.22) | collective-permute-done | bytes 4194336 | tf_op jit(solution)/shard_map/ppermute | solution.py:270
  871.6 3.2 copy-done.4
  877.1 15.6 %finish.1 = bf16[1024,2048]{1,0:T(8,128)(2,1)} custom-call(bf16[1024,2048]{1,0:T(8,128)(2,1)S(1)} %copy-done.2, f32[1024,16,128]{2,1,0:T(8,128)} %get-tuple-element.29.mine_ref, f32[1024,16,128]{2,1,0:T(8,128)} %copy-done.4, f32[512,16,128]{2,1,0:T(8,128)} %copy-done.5, f32[512,16,128]{2,1,0:T(8,128)} %copy-done.6, f32[512,16,128]{2,1,0:T(8,128)} %copy-done.7, ...), custom_call_target="tpu_custom_call" | custom-call | flops 16777216 | bytes 41943040 | tf_op jit(solution)/shard_map/finish/pallas_call | solution.py:195
  (121 shorter events, 42.3 us)
Async XLA Ops:
  36.8 48.3 %collective-permute-start.6 = (bf16[512,16,128]{2,1,0:T(8,128)(2,1)S(1)}, bf16[512,16,128]{2,1,0:T(8,128)(2,1)}, u32[]{:S(2)}, u32[]{:S(2)}) collective-permute-start(bf16[512,16,128]{2,1,0:T(8,128)(2,1)S(1)} %bitcast.142), channel_id=1, source_target_pairs={{0,2},{1,3},{2,4},{3,5},{4,6},{5,7},{6,0},{7,1},{8,10},{9,11},{10,... | collective-permute-start | bytes 6291464 | tf_op jit(solution)/shard_map/ppermute | solution.py:270
  37.8 48.3 %collective-permute-start.8 = (bf16[512,16,128]{2,1,0:T(8,128)(2,1)}, bf16[512,16,128]{2,1,0:T(8,128)(2,1)}, u32[]{:S(2)}, u32[]{:S(2)}) collective-permute-start(bf16[512,16,128]{2,1,0:T(8,128)(2,1)} %bitcast.73.seg_b), channel_id=1, source_target_pairs={{0,6},{1,7},{2,0},{3,1},{4,2},{5,3},{6,4},{7,5},{8,14},{9,15},{10,... | collective-permute-start | bytes 6291464 | tf_op jit(solution)/shard_map/ppermute | solution.py:270
  85.1 24.8 %collective-permute-start.12 = (bf16[512,16,128]{2,1,0:T(8,128)(2,1)}, bf16[512,16,128]{2,1,0:T(8,128)(2,1)}, u32[]{:S(2)}, u32[]{:S(2)}) collective-permute-start(bf16[512,16,128]{2,1,0:T(8,128)(2,1)} %collective-permute-done.6.seg_a), channel_id=1, source_target_pairs={{0,1},{1,0},{2,3},{3,2},{4,5},{5,4},{6,7},{7,6},{8,9},{9,8},{10,11... | collective-permute-start | bytes 6291464 | tf_op jit(solution)/shard_map/ppermute | solution.py:270
  86.1 23.7 %collective-permute-start.13 = (bf16[512,16,128]{2,1,0:T(8,128)(2,1)}, bf16[512,16,128]{2,1,0:T(8,128)(2,1)}, u32[]{:S(2)}, u32[]{:S(2)}) collective-permute-start(bf16[512,16,128]{2,1,0:T(8,128)(2,1)} %collective-permute-done.8.seg_b), channel_id=1, source_target_pairs={{0,1},{1,0},{2,3},{3,2},{4,5},{5,4},{6,7},{7,6},{8,9},{9,8},{10,11... | collective-permute-start | bytes 6291464 | tf_op jit(solution)/shard_map/ppermute | solution.py:270
  182.7 74.2 %collective-permute-start.14 = (f32[1024,16,128]{2,1,0:T(8,128)}, f32[1024,16,128]{2,1,0:T(8,128)}, u32[]{:S(2)}, u32[]{:S(2)}) collective-permute-start(f32[1024,16,128]{2,1,0:T(8,128)} %get-tuple-element.24), channel_id=1, source_target_pairs={{0,1},{1,0},{2,3},{3,2},{4,5},{5,4},{6,7},{7,6},{8,9},{9,8},{10,11... | collective-permute-start | bytes 25165832 | tf_op jit(solution)/shard_map/ppermute | solution.py:270
  184.0 52.2 %collective-permute-start.7 = (bf16[512,16,128]{2,1,0:T(8,128)(2,1)}, bf16[512,16,128]{2,1,0:T(8,128)(2,1)S(1)}, u32[]{:S(2)}, u32[]{:S(2)}) collective-permute-start(bf16[512,16,128]{2,1,0:T(8,128)(2,1)} %collective-permute-done.6.seg_a), channel_id=1, source_target_pairs={{0,2},{1,3},{2,4},{3,5},{4,6},{5,7},{6,0},{7,1},{8,10},{9,11},{10,... | collective-permute-start | bytes 6291464 | tf_op jit(solution)/shard_map/ppermute | solution.py:270
  188.9 48.2 %collective-permute-start.9 = (bf16[512,16,128]{2,1,0:T(8,128)(2,1)}, bf16[512,16,128]{2,1,0:T(8,128)(2,1)}, u32[]{:S(2)}, u32[]{:S(2)}) collective-permute-start(bf16[512,16,128]{2,1,0:T(8,128)(2,1)} %collective-permute-done.8.seg_b), channel_id=1, source_target_pairs={{0,6},{1,7},{2,0},{3,1},{4,2},{5,3},{6,4},{7,5},{8,14},{9,15},{10,... | collective-permute-start | bytes 6291464 | tf_op jit(solution)/shard_map/ppermute | solution.py:270
  236.2 30.9 %collective-permute-start.10 = (bf16[512,16,128]{2,1,0:T(8,128)(2,1)S(1)}, bf16[512,16,128]{2,1,0:T(8,128)(2,1)}, u32[]{:S(2)}, u32[]{:S(2)}) collective-permute-start(bf16[512,16,128]{2,1,0:T(8,128)(2,1)S(1)} %collective-permute-done.7.seg_a), channel_id=1, source_target_pairs={{0,1},{1,0},{2,3},{3,2},{4,5},{5,4},{6,7},{7,6},{8,9},{9,8},{10,11... | collective-permute-start | bytes 6291464 | tf_op jit(solution)/shard_map/ppermute | solution.py:270
  237.2 30.0 %collective-permute-start.11 = (bf16[512,16,128]{2,1,0:T(8,128)(2,1)}, bf16[512,16,128]{2,1,0:T(8,128)(2,1)}, u32[]{:S(2)}, u32[]{:S(2)}) collective-permute-start(bf16[512,16,128]{2,1,0:T(8,128)(2,1)} %collective-permute-done.9.seg_b), channel_id=1, source_target_pairs={{0,1},{1,0},{2,3},{3,2},{4,5},{5,4},{6,7},{7,6},{8,9},{9,8},{10,11... | collective-permute-start | bytes 6291464 | tf_op jit(solution)/shard_map/ppermute | solution.py:270
  339.8 63.3 %collective-permute-start.15 = (f32[1024,16,128]{2,1,0:T(8,128)}, f32[1024,16,128]{2,1,0:T(8,128)}, u32[]{:S(2)}, u32[]{:S(2)}) collective-permute-start(f32[1024,16,128]{2,1,0:T(8,128)} %get-tuple-element.26), channel_id=1, source_target_pairs={{0,1},{1,0},{2,3},{3,2},{4,5},{5,4},{6,7},{7,6},{8,9},{9,8},{10,11... | collective-permute-start | bytes 25165832 | tf_op jit(solution)/shard_map/ppermute | solution.py:270
  352.4 48.5 %collective-permute-start.2 = (bf16[512,16,128]{2,1,0:T(8,128)(2,1)}, bf16[512,16,128]{2,1,0:T(8,128)(2,1)S(1)}, u32[]{:S(2)}, u32[]{:S(2)}) collective-permute-start(bf16[512,16,128]{2,1,0:T(8,128)(2,1)} %bitcast.73.seg_b), channel_id=1, source_target_pairs={{0,2},{1,3},{2,4},{3,5},{4,6},{5,7},{6,0},{7,1},{8,10},{9,11},{10,... | collective-permute-start | bytes 6291464 | tf_op jit(solution)/shard_map/ppermute | solution.py:270
  352.4 49.5 %collective-permute-start.3 = (bf16[512,16,128]{2,1,0:T(8,128)(2,1)}, bf16[512,16,128]{2,1,0:T(8,128)(2,1)}, u32[]{:S(2)}, u32[]{:S(2)}) collective-permute-start(bf16[512,16,128]{2,1,0:T(8,128)(2,1)} %bitcast.143), channel_id=1, source_target_pairs={{0,6},{1,7},{2,0},{3,1},{4,2},{5,3},{6,4},{7,5},{8,14},{9,15},{10,... | collective-permute-start | bytes 6291464 | tf_op jit(solution)/shard_map/ppermute | solution.py:270
  400.8 12.5 %collective-permute-start.4 = (bf16[512,16,128]{2,1,0:T(8,128)(2,1)S(1)}, bf16[512,16,128]{2,1,0:T(8,128)(2,1)}, u32[]{:S(2)}, u32[]{:S(2)}) collective-permute-start(bf16[512,16,128]{2,1,0:T(8,128)(2,1)S(1)} %collective-permute-done.2.seg_a), channel_id=1, source_target_pairs={{0,1},{1,0},{2,3},{3,2},{4,5},{5,4},{6,7},{7,6},{8,9},{9,8},{10,11... | collective-permute-start | bytes 6291464 | tf_op jit(solution)/shard_map/ppermute | solution.py:270
  401.8 11.5 %collective-permute-start.5 = (bf16[512,16,128]{2,1,0:T(8,128)(2,1)}, bf16[512,16,128]{2,1,0:T(8,128)(2,1)}, u32[]{:S(2)}, u32[]{:S(2)}) collective-permute-start(bf16[512,16,128]{2,1,0:T(8,128)(2,1)} %collective-permute-done.3.seg_b), channel_id=1, source_target_pairs={{0,1},{1,0},{2,3},{3,2},{4,5},{5,4},{6,7},{7,6},{8,9},{9,8},{10,11... | collective-permute-start | bytes 6291464 | tf_op jit(solution)/shard_map/ppermute | solution.py:270
  492.0 94.6 %collective-permute-start.16 = (f32[1024,16,128]{2,1,0:T(8,128)}, f32[1024,16,128]{2,1,0:T(8,128)}, u32[]{:S(2)}, u32[]{:S(2)}) collective-permute-start(f32[1024,16,128]{2,1,0:T(8,128)} %get-tuple-element.28), channel_id=1, source_target_pairs={{0,1},{1,0},{2,3},{3,2},{4,5},{5,4},{6,7},{7,6},{8,9},{9,8},{10,11... | collective-permute-start | bytes 25165832 | tf_op jit(solution)/shard_map/ppermute | solution.py:270
  493.1 92.3 %collective-permute-start.17 = (f32[512,16,128]{2,1,0:T(8,128)}, f32[512,16,128]{2,1,0:T(8,128)}, u32[]{:S(2)}, u32[]{:S(2)}) collective-permute-start(f32[512,16,128]{2,1,0:T(8,128)} %get-tuple-element.40.refs_0_), channel_id=1, source_target_pairs={{0,6},{1,7},{2,0},{3,1},{4,2},{5,3},{6,4},{7,5},{8,14},{9,15},{10,... | collective-permute-start | bytes 12582920 | tf_op jit(solution)/shard_map/ppermute | solution.py:270
  493.1 93.4 %collective-permute-start.18 = (f32[512,16,128]{2,1,0:T(8,128)}, f32[512,16,128]{2,1,0:T(8,128)}, u32[]{:S(2)}, u32[]{:S(2)}) collective-permute-start(f32[512,16,128]{2,1,0:T(8,128)} %get-tuple-element.39.refs_1_), channel_id=1, source_target_pairs={{0,2},{1,3},{2,4},{3,5},{4,6},{5,7},{6,0},{7,1},{8,10},{9,11},{10,... | collective-permute-start | bytes 12582920 | tf_op jit(solution)/shard_map/ppermute | solution.py:270
  494.6 104.6 %collective-permute-start = (bf16[512,16,128]{2,1,0:T(8,128)(2,1)}, bf16[512,16,128]{2,1,0:T(8,128)(2,1)}, u32[]{:S(2)}, u32[]{:S(2)}) collective-permute-start(bf16[512,16,128]{2,1,0:T(8,128)(2,1)} %bitcast.144), channel_id=1, source_target_pairs={{0,1},{1,0},{2,3},{3,2},{4,5},{5,4},{6,7},{7,6},{8,9},{9,8},{10,11... | collective-permute-start | bytes 6291464 | tf_op jit(solution)/shard_map/ppermute | solution.py:270
  495.3 103.9 %collective-permute-start.1 = (bf16[512,16,128]{2,1,0:T(8,128)(2,1)}, bf16[512,16,128]{2,1,0:T(8,128)(2,1)}, u32[]{:S(2)}, u32[]{:S(2)}) collective-permute-start(bf16[512,16,128]{2,1,0:T(8,128)(2,1)} %bitcast.73.seg_b), channel_id=1, source_target_pairs={{0,1},{1,0},{2,3},{3,2},{4,5},{5,4},{6,7},{7,6},{8,9},{9,8},{10,11... | collective-permute-start | bytes 6291464 | tf_op jit(solution)/shard_map/ppermute | solution.py:270
  683.7 184.7 %collective-permute-start.19 = (f32[1024,16,128]{2,1,0:T(8,128)}, f32[1024,16,128]{2,1,0:T(8,128)S(1)}, u32[]{:S(2)}, u32[]{:S(2)}) collective-permute-start(f32[1024,16,128]{2,1,0:T(8,128)} %get-tuple-element.30), channel_id=1, source_target_pairs={{0,1},{1,0},{2,3},{3,2},{4,5},{5,4},{6,7},{7,6},{8,9},{9,8},{10,11... | collective-permute-start | bytes 25165832 | tf_op jit(solution)/shard_map/ppermute | solution.py:270
  685.2 92.2 %collective-permute-start.20 = (f32[512,16,128]{2,1,0:T(8,128)}, f32[512,16,128]{2,1,0:T(8,128)S(1)}, u32[]{:S(2)}, u32[]{:S(2)}) collective-permute-start(f32[512,16,128]{2,1,0:T(8,128)} %get-tuple-element.42.refs_0_), channel_id=1, source_target_pairs={{0,6},{1,7},{2,0},{3,1},{4,2},{5,3},{6,4},{7,5},{8,14},{9,15},{10,... | collective-permute-start | bytes 12582920 | tf_op jit(solution)/shard_map/ppermute | solution.py:270
  685.2 93.3 %collective-permute-start.21 = (f32[512,16,128]{2,1,0:T(8,128)}, f32[512,16,128]{2,1,0:T(8,128)S(1)}, u32[]{:S(2)}, u32[]{:S(2)}) collective-permute-start(f32[512,16,128]{2,1,0:T(8,128)} %get-tuple-element.41.refs_1_), channel_id=1, source_target_pairs={{0,2},{1,3},{2,4},{3,5},{4,6},{5,7},{6,0},{7,1},{8,10},{9,11},{10,... | collective-permute-start | bytes 12582920 | tf_op jit(solution)/shard_map/ppermute | solution.py:270
  686.6 181.7 %collective-permute-start.22 = (f32[512,16,128]{2,1,0:T(8,128)}, f32[512,16,128]{2,1,0:T(8,128)S(1)}, u32[]{:S(2)}, u32[]{:S(2)}) collective-permute-start(f32[512,16,128]{2,1,0:T(8,128)} %get-tuple-element.37.refs_1_), channel_id=1, source_target_pairs={{0,2},{1,3},{2,4},{3,5},{4,6},{5,7},{6,0},{7,1},{8,10},{9,11},{10,... | collective-permute-start | bytes 12582920 | tf_op jit(solution)/shard_map/ppermute | solution.py:270
  686.7 181.7 %collective-permute-start.23 = (f32[512,16,128]{2,1,0:T(8,128)}, f32[512,16,128]{2,1,0:T(8,128)S(1)}, u32[]{:S(2)}, u32[]{:S(2)}) collective-permute-start(f32[512,16,128]{2,1,0:T(8,128)} %get-tuple-element.38.refs_0_), channel_id=1, source_target_pairs={{0,6},{1,7},{2,0},{3,1},{4,2},{5,3},{6,4},{7,5},{8,14},{9,15},{10,... | collective-permute-start | bytes 12582920 | tf_op jit(solution)/shard_map/ppermute | solution.py:270
  (16 other events, 567.1 us)
Sparse Core Ops, SparseCore 0:
  42.4 22.4 sort.19.cloned.1.call-done
  (1 shorter events, 0.0 us)

commit v2 on v1

v2 whole, which is shorter than its diff:
```python
import functools

import jax
import jax.numpy as jnp
from jax import lax
from jax.experimental import pallas as pl
from jax.experimental.pallas import tpu as pltpu
from jax.sharding import PartitionSpec as P


LANES = 128
ROW_SIZES = (160, 208, 256, 320)
MANY_ROWS = ROW_SIZES[-1]
PITCH = MANY_ROWS + 12
SLAB = 24
CHUNK = 256
SLOTS = 3


def capacity_of(tok_dev, top_k, num_exp):
    base_load = tok_dev * top_k // num_exp
    return base_load + base_load // 2 + min(tok_dev * top_k % num_exp, 1)


def experts_kernel(list_cap, num_after, count_s, tok_s, gate_s, seg_a, seg_b, seg_c, seg_d, w_gate, w_up, w_down, *refs):
    (*outs, tok_v, acc, buf_g, buf_u, buf_d, slab_v, rows_v, hid_v,
     sem_tok, sem_g, sem_u, sem_d, sem_out) = refs[num_after:]
    slots, width = buf_d.shape[:2]
    num_loc, model_dim, ff_dim = w_gate.shape
    half = seg_a.shape[0]
    pieces = seg_a.shape[1]
    segs = (seg_a, seg_b, seg_c, seg_d)
    num_segs = len(segs)
    num_rows = num_segs * half

    parts = [(start, min(width, ff_dim - start)) for start in range(0, ff_dim, width)]

    def load(stage, part):
        exp, slot = stage // len(parts), lax.rem(stage, slots)
        start, cols = parts[part]
        return (pltpu.make_async_copy(w_gate.at[exp, :, pl.ds(start, cols)], buf_g.at[slot, :, pl.ds(0, cols)], sem_g.at[slot]),
                pltpu.make_async_copy(w_up.at[exp, :, pl.ds(start, cols)], buf_u.at[slot, :, pl.ds(0, cols)], sem_u.at[slot]),
                pltpu.make_async_copy(w_down.at[exp, pl.ds(start, cols)], buf_d.at[slot, pl.ds(0, cols)], sem_d.at[slot]))

    seg_copies = [pltpu.make_async_copy(seg, tok_v.at[pl.ds(half * idx, half)], sem_tok.at[idx]) for idx, seg in enumerate(segs)]
    for copy in seg_copies:
        copy.start()
    for copy in load(0, 0):
        copy.start()

    def clear(idx, carry):
        acc[pl.ds(idx * 8, 8)] = jnp.zeros((8, pieces, LANES), jnp.float32)
        return carry

    lax.fori_loop(0, num_rows // 8, clear, 0)
    tok_v[num_rows] = jnp.zeros((pieces, LANES), jnp.bfloat16)
    acc[num_rows] = jnp.zeros((pieces, LANES), jnp.float32)
    for copy in seg_copies:
        copy.wait()
    for stage in range(1, slots):
        for copy in load(stage, stage % len(parts)):
            copy.start()

    def unpack(rows):
        for col in range(pieces):
            rows_v[:rows, col * LANES:(col + 1) * LANES] = slab_v[col * PITCH:col * PITCH + rows, :].astype(jnp.bfloat16)

    def multiply(slot, part, rows):
        cols = parts[part][1]
        if part == 0:
            unpack(rows)
        for start in range(0, cols, CHUNK):
            span = slice(start, min(start + CHUNK, cols))
            gate_act = jnp.dot(rows_v[:rows], buf_g[slot, :, span], preferred_element_type=jnp.float32)
            up_act = jnp.dot(rows_v[:rows], buf_u[slot, :, span], preferred_element_type=jnp.float32)
            hid_v[:rows, span] = (jax.nn.silu(gate_act) * up_act).astype(jnp.bfloat16)
        for start in range(0, model_dim, CHUNK):
            out_rows = jnp.dot(hid_v[:rows, :cols], buf_d[slot, :cols, start:start + CHUNK], preferred_element_type=jnp.float32)
            for off in range(0, CHUNK, LANES):
                place = pl.ds((start + off) // LANES * PITCH, rows)
                piece = out_rows[:, off:off + LANES]
                if part > 0:
                    piece = slab_v[place, :] + piece
                if part == len(parts) - 1:
                    piece = piece.astype(jnp.bfloat16).astype(jnp.float32)
                slab_v[place, :] = piece

    def expert(exp, carry):
        counts = [count_s[exp * num_segs + seg] for seg in range(num_segs)]
        total = functools.reduce(lambda left, right: left + right, counts)
        whole = total <= MANY_ROWS
        num_blocks = jnp.where(whole, 1, 2)

        def block(blk, carry):
            pair = num_segs // 2
            first = jnp.where(whole, 0, pair * blk)
            last = jnp.where(whole, num_segs, pair * blk + pair)
            rows = jnp.where(whole, total, jnp.where(blk == 0, counts[0] + counts[1], counts[2] + counts[3]))

            def lists(body):
                def one(seg, offset):
                    index = exp * num_segs + seg
                    base = index * list_cap
                    count = count_s[index]

                    def step(grp, carry):
                        body(base + grp * 8, offset + grp * 8)
                        return carry

                    lax.fori_loop(0, (count + 7) // 8, step, 0)
                    return offset + count

                lax.fori_loop(first, last, one, 0)

            def fetch(base, row):
                for lane in range(8):
                    slab_v[pl.ds(row + lane, pieces, stride=PITCH), :] = tok_v[tok_s[base + lane]].astype(jnp.float32)

            lists(fetch)

            for part in range(len(parts)):
                stage = exp * len(parts) + part
                slot = lax.rem(stage, slots)

                @pl.when(blk == 0)
                def _():
                    for copy in load(stage, part):
                        copy.wait()

                for low, size in zip((-1,) + ROW_SIZES[:-1], ROW_SIZES):
                    pl.when((rows > low) & (rows <= size))(functools.partial(multiply, slot, part, size))

                @pl.when((blk == num_blocks - 1) & (stage + slots < num_loc * len(parts)))
                def _():
                    for copy in load(stage + slots, (part + slots) % len(parts)):
                        copy.start()

            def combine(base, row):
                toks, sums = [], []
                for lane in range(8):
                    tok = tok_s[base + lane]
                    piece = slab_v[pl.ds(row + lane, pieces, stride=PITCH), :]
                    toks.append(tok)
                    sums.append(acc[tok] + gate_s[base + lane] * piece)
                for tok, val in zip(toks, sums):
                    acc[tok] = val

            lists(combine)
            return carry

        lax.fori_loop(0, num_blocks, block, 0)
        return carry

    lax.fori_loop(0, num_loc, expert, 0)
    out_copies = [pltpu.make_async_copy(acc.at[pl.ds(half * idx, half)], out, sem_out.at[idx]) for idx, out in enumerate(outs)]
    for copy in out_copies:
        copy.start()
    for copy in out_copies:
        copy.wait()


def expert_pass(counts, toks, gates, segs, w_gate, w_up, w_down, list_cap, after):
    num_loc, model_dim, ff_dim = w_gate.shape
    half, pieces, _ = segs[0].shape
    num_rows = 4 * half
    out_type = jax.ShapeDtypeStruct((half, pieces, LANES), jnp.float32)
    any_spec = pl.BlockSpec(memory_space=pl.ANY)
    smem_spec = pl.BlockSpec(memory_space=pltpu.SMEM)
    avg_rows = num_rows * 6 // 8
    part_dim = -(-ff_dim // (2 * CHUNK)) * CHUNK
    return pl.pallas_call(
        functools.partial(experts_kernel, list_cap, len(after)),
        out_shape=(out_type,) * len(segs),
        in_specs=[smem_spec] * 3 + [any_spec] * (7 + len(after)),
        out_specs=(any_spec,) * len(segs),
        scratch_shapes=[
            pltpu.VMEM((num_rows + 8, pieces, LANES), jnp.bfloat16),
            pltpu.VMEM((num_rows + 8, pieces, LANES), jnp.float32),
            pltpu.VMEM((SLOTS, model_dim, part_dim), jnp.bfloat16),
            pltpu.VMEM((SLOTS, model_dim, part_dim), jnp.bfloat16),
            pltpu.VMEM((SLOTS, part_dim, model_dim), jnp.bfloat16),
            pltpu.VMEM((pieces * PITCH, LANES), jnp.float32),
            pltpu.VMEM((MANY_ROWS, model_dim), jnp.bfloat16),
            pltpu.VMEM((MANY_ROWS, part_dim), jnp.bfloat16),
            pltpu.SemaphoreType.DMA((4,)),
            pltpu.SemaphoreType.DMA((SLOTS,)),
            pltpu.SemaphoreType.DMA((SLOTS,)),
            pltpu.SemaphoreType.DMA((SLOTS,)),
            pltpu.SemaphoreType.DMA((4,)),
        ],
        compiler_params=pltpu.CompilerParams(vmem_limit_bytes=63 * 1024 * 1024),
        cost_estimate=pl.CostEstimate(flops=6 * avg_rows * model_dim * ff_dim * 3 // 2, transcendentals=0,
                                      bytes_accessed=3 * num_loc * model_dim * ff_dim * 2),
        name='experts',
    )(counts, toks, gates, *segs, w_gate, w_up, w_down, *after)


def merge_kernel(blocks_half, num_pairs, *refs):
    base_ref, out_ref, sum_v = refs[0], refs[-2], refs[-1]
    rows = base_ref.shape[0]
    pieces = refs[1].shape[1]
    idx = pl.program_id(0)

    def add_up(side):
        total = refs[1 + side][...]
        for pair in range(1, num_pairs):
            total = total + refs[1 + 2 * pair + side][...]
        for row in range(rows):
            sum_v[row * SLAB:row * SLAB + pieces, :] = total[row]

    pl.when(idx < blocks_half)(lambda: add_up(0))
    pl.when(idx >= blocks_half)(lambda: add_up(1))
    for col in range(pieces):
        cols = slice(col * LANES, (col + 1) * LANES)
        out_ref[:, cols] = (base_ref[:, cols].astype(jnp.float32) + sum_v[pl.ds(col, rows, stride=SLAB), :]).astype(out_ref.dtype)


def merge(base, pairs, out_dtype):
    tok_dev, model_dim = base.shape
    pieces = pairs[0][0].shape[1]
    rows = 128
    blocks_half = tok_dev // rows // 2
    slab = (rows, pieces, LANES)
    flat_spec = pl.BlockSpec((rows, model_dim), lambda idx: (idx, 0))
    first_spec = pl.BlockSpec(slab, lambda idx: (jnp.minimum(idx, blocks_half - 1), 0, 0))
    second_spec = pl.BlockSpec(slab, lambda idx: (jnp.maximum(idx - blocks_half, 0), 0, 0))
    return pl.pallas_call(
        functools.partial(merge_kernel, blocks_half, len(pairs)),
        out_shape=jax.ShapeDtypeStruct((tok_dev, model_dim), out_dtype),
        grid=(tok_dev // rows,),
        in_specs=[flat_spec] + [first_spec, second_spec] * len(pairs),
        out_specs=flat_spec,
        scratch_shapes=[pltpu.VMEM((rows * SLAB, LANES), jnp.float32)],
        compiler_params=pltpu.CompilerParams(vmem_limit_bytes=62 * 1024 * 1024),
        cost_estimate=pl.CostEstimate(flops=tok_dev * model_dim * 8, transcendentals=0, bytes_accessed=tok_dev * model_dim * 16),
        name='add_up',
    )(base, *[part for pair in pairs for part in pair])


def routing_exchange(tok_rows, w_router, ids_loc):
    top_k = ids_loc.shape[1]
    num_exp = w_router.shape[1]
    logits = lax.dot_general(w_router, tok_rows, (((0,), (1,)), ((), ())), preferred_element_type=jnp.float32)
    ids = ids_loc.T
    exp_range = jnp.arange(num_exp, dtype=jnp.int32)[:, None]
    picked = jnp.stack([jnp.sum(jnp.where(ids[k][None, :] == exp_range, logits, 0.0), axis=0) for k in range(top_k)])
    gates = jax.nn.softmax(picked, axis=0)
    packed = jnp.concatenate([ids.astype(jnp.float32), gates], axis=0)
    return lax.all_gather(packed, 'ep')


def routing_tables(everyone, num_exp, group, list_cap):
    top_k, tok_dev = everyone.shape[1] // 2, everyone.shape[2]
    num_loc = num_exp // group
    half = tok_dev // 2
    me = lax.axis_index('ep')
    chip, core = me // 2, me % 2
    chips = group // 2
    order = [((chip + off) % chips) * 2 + side for off in range(chips) for side in (core, 1 - core)]
    rolled = [lax.dynamic_index_in_dim(everyone, src, 0, keepdims=False) for src in order]
    passes = [[(6, 0), (2, 1), (7, 0), (3, 1)],
              [(4, 0), (4, 1), (5, 0), (5, 1)],
              [(6, 1), (2, 0), (7, 1), (3, 0)],
              [(0, 0), (0, 1), (1, 0), (1, 1)]]
    num_segs = len(passes[0])
    halves = jnp.stack([rolled[src][:, side * half:(side + 1) * half] for segs in passes for src, side in segs])
    halves = halves.reshape(len(passes), 1, num_segs, 2 * top_k, half)
    mine = (me * num_loc + jnp.arange(num_loc, dtype=jnp.int32)).astype(jnp.float32)[None, :, None, None]
    columns = (len(passes), num_loc, num_segs, half)
    named = jnp.zeros(columns, jnp.bool_)
    gate = jnp.zeros(columns, jnp.float32)
    for k in range(top_k):
        hit = halves[:, :, :, k] == mine
        named = named | hit
        gate = gate + jnp.where(hit, halves[:, :, :, top_k + k], 0.0)
    counts = jnp.sum(named.astype(jnp.int32), axis=3).reshape(len(passes), num_loc * num_segs)
    place = jnp.arange(half, dtype=jnp.int32) + half * jnp.arange(num_segs, dtype=jnp.int32)[:, None]
    key = jnp.where(named, place[None, None], half * num_segs)
    flat = (len(passes) * num_loc * num_segs, half)
    key, gate = lax.sort((key.reshape(flat).T, gate.reshape(flat).T), dimension=0, num_keys=1, is_stable=False)
    lists = (len(passes), num_loc * num_segs * list_cap)
    return counts, key[:list_cap].T.reshape(lists), gate[:list_cap].T.reshape(lists)


def solution(mesh):
    group = mesh.shape['ep']
    row_spec = P(('dp', 'ep'), None)
    full_spec = P(None, None)
    expert_spec = P('ep', None, None)
    forward = [(dev, (dev + 2) % group) for dev in range(group)]
    backward = [(dev, (dev - 2) % group) for dev in range(group)]
    across = [(dev, dev ^ 1) for dev in range(group)]

    def send(array, route):
        return lax.ppermute(array, 'ep', route)

    def device_step(tok_rows, w_router, ids_loc, w_gate, w_up, w_down, shared_gate, shared_up, shared_down):
        tok_dev, model_dim = tok_rows.shape
        top_k = ids_loc.shape[1]
        num_exp = w_router.shape[1]
        half = tok_dev // 2
        pieces = model_dim // LANES
        list_cap = -(-capacity_of(tok_dev, top_k, num_exp) // 8) * 8
        slabs = tok_rows.reshape(tok_dev, pieces, LANES)
        own_a, own_b = slabs[:half], slabs[half:]
        everyone = routing_exchange(tok_rows, w_router, ids_loc)
        left_a = send(own_a, forward)
        right_b = send(own_b, backward)
        pair_a, pair_b = send(own_a, across), send(own_b, across)
        counts, toks, gates = routing_tables(everyone, num_exp, group, list_cap)

        def run(idx, segs, after):
            mine_a, mine_b, other_a, other_b = expert_pass(counts[idx], toks[idx], gates[idx], segs, w_gate, w_up, w_down, list_cap, after)
            return mine_a, mine_b, send(other_a, across), send(other_b, across)

        gate_act = jnp.dot(tok_rows, shared_gate, preferred_element_type=jnp.float32)
        up_act = jnp.dot(tok_rows, shared_up, preferred_element_type=jnp.float32)
        hidden = (jax.nn.silu(gate_act) * up_act).astype(jnp.bfloat16)
        shared_out = jnp.dot(hidden, shared_down, preferred_element_type=jnp.float32).astype(jnp.bfloat16)

        far_a, far_b = send(left_a, forward), send(right_b, backward)
        left_b, right_a = send(own_b, forward), send(own_a, backward)

        segs = [left_a, right_b, send(left_a, across), send(right_b, across)]
        mine_a, mine_b, other_a, other_b = run(0, segs, [hidden])
        to_left, to_right = mine_a + other_a, mine_b + other_b
        near_a, near_b = send(to_left, backward), send(to_right, forward)

        segs = [far_a, far_b, send(far_a, across), send(far_b, across)]
        mine_a, mine_b, other_a, other_b = run(1, segs, [to_left, to_right])
        to_right, to_left = mine_a + other_a, mine_b + other_b
        via_a, via_b = send(to_right, forward), send(to_left, backward)

        segs = [left_b, right_a, send(left_b, across), send(right_a, across)]
        mine_a, mine_b, other_a, other_b = run(2, segs, [to_left, to_right])
        to_left, to_right = mine_a + other_a + via_b, mine_b + other_b + via_a
        last_b, last_a = send(to_left, backward), send(to_right, forward)

        mine_a, mine_b, other_a, other_b = run(3, [own_a, own_b, pair_a, pair_b], [to_left, to_right, shared_out])
        total = merge(shared_out, [(near_a, near_b)], jnp.float32)
        return merge(total, [(mine_a, mine_b), (other_a, other_b), (last_a, last_b)], jnp.bfloat16)

    return jax.shard_map(device_step, mesh=mesh, in_specs=(row_spec, full_spec, row_spec, expert_spec, expert_spec, expert_spec, full_spec, full_spec, full_spec), out_specs=row_spec, check_vma=False)
```

time: 905 us -> 771 us (0.85)
  waiting for transfers between devices: 383 us -> 258 us
  Pallas kernels: 324 us -> 273 us
  blocking collectives: 15.1 us -> 50.3 us
  local copies, waits for them, and re-layouts: 30.1 us -> 44.7 us
  between operations: 14.1 us -> 0.75 us
    ppermute x24 -> x28, waiting for transfers between devices: 383 us -> 258 us  [send(): return lax.ppermute(array, 'ep', route)]
    pallas_call x5 -> x6, Pallas kernels: 324 us -> 273 us  [the longest x4 248 us: expert_pass(): pl.pallas_call(functools.partial(experts_kernel, list_cap, len(after)), o...]
    all_gather x1, blocking collectives: 15.1 us -> 50.3 us  [routing_exchange(): return lax.all_gather(packed, 'ep')]
    eq x0 -> x14, local copies, waits for them, and re-layouts: none -> 16.6 us  [routing_tables(): hit = halves[:, :, :, k] == mine]
    unnamed x47 -> x37, local copies, waits for them, and re-layouts: 20.5 us -> 6.62 us
    broadcast_in_dim x0 -> x15, local copies, waits for them, and re-layouts: none -> 10.2 us  [the longest x13 7.69 us: routing_tables(): gate = gate + jnp.where(hit, halves[:, :, :, top_k + k], 0.0)]
    ppermute x24 -> x28, starting transfers between devices: 38.2 us -> 29.8 us  [send(): return lax.ppermute(array, 'ep', route)]
    add x4 -> x7, other arithmetic: 33.2 us -> 36.5 us  [the longest x2 13.9 us: device_step(): to_left, to_right = (mine_a + other_a + via_b, mine_b + other_b + via_a)]
  transfers between devices with their start and end apart: 24 -> 28, of which waited for: 8 -> 8; matrix products, arithmetic and copies ran while one was open for 11% -> 19% of each run, Pallas kernels for 0% -> 10%
where the time goes in v2:
time: 771 us; the launch traced here: 762 us
  Pallas kernels  273 us (35%)
  waiting for transfers between devices  258 us (33%)
  matrix products  60.6 us (8%)
  blocking collectives  50.3 us (7%)
  other arithmetic  44.9 us (6%)
  local copies, waits for them, and re-layouts  44.7 us (6%)
  starting transfers between devices  29.8 us (4%)
    ppermute x28, waiting for transfers between devices, send(): return lax.ppermute(array, 'ep', route)  258 us
    pallas_call x4, Pallas kernels, expert_pass(): pl.pallas_call(functools.partial(experts_kernel, list_cap, len(after)), o...  248 us
    all_gather x1, blocking collectives, routing_exchange(): return lax.all_gather(packed, 'ep')  50.3 us
    ppermute x28, starting transfers between devices, send(): return lax.ppermute(array, 'ep', route)  29.8 us
    pallas_call x2, Pallas kernels, merge(): pl.pallas_call(functools.partial(merge_kernel, blocks_half, len(pairs)),...  25.4 us
    dot_general x1, matrix products, device_step(): jnp.dot(tok_rows, shared_gate, preferred_element_type=jnp.float32)  19.7 us
    dot_general x1, matrix products, device_step(): up_act = jnp.dot(tok_rows, shared_up, preferred_element_type=jnp.float32)  19.1 us
    dot_general x1, matrix products, device_step(): jnp.dot(hidden, shared_down, preferred_element_type=jnp.float32)  18 us
  transfers between devices with their start and end apart: 28, of which 8 were waited for; matrix products, arithmetic and copies ran while one was open for 19% of the time, Pallas kernels for 10%

profile of v2, /device:TPU:81, one launch (start us, length us, event | category | flops | bytes accessed | tf_op | source)
XLA Modules:
  0.0 761.7 jit_solution(16328357344163340367)
XLA Ops:
  13.8 50.3 %all-gather.1 = f32[8,12,1024]{2,1,0:T(8,128)S(1)} all-gather(f32[1,12,1024]{2,1,0:T(8,128)S(1)} %maximum_bitcast_fusion), channel_id=2, replica_groups=mesh['dp'=4,'ep'=8] {'ep'}, dimensions={0}, use_global_device_ids=true | all-gather | bytes 442368 | tf_op jit(solution)/shard_map/all_gather | solution.py:249
  106.1 19.7 %fusion.14 = f32[1024,2816]{1,0:T(8,128)} fusion(bf16[1024,2048]{1,0:T(8,128)(2,1)} %param.9, bf16[2048,2816]{1,0:T(8,128)(2,1)} %param.15), kind=kOutput, calls=%fused_computation.78 | convolution fusion | flops 11811160064 | bytes 27262976 | tf_op jit(solution)/shard_map/dot_general | solution.py:316
  126.3 19.1 %multiply_convert_fusion.refs_0_ = bf16[1024,2816]{1,0:T(8,128)(2,1)} fusion(f32[1024,2816]{1,0:T(8,128)} %fusion.14, bf16[1024,2048]{1,0:T(8,128)(2,1)S(1)} %copy-done.5, bf16[2048,2816]{1,0:T(8,128)(2,1)} %param.16), kind=kOutput, calls=%fused_computation | convolution fusion | flops 11828461568 | bytes 33030144 | tf_op jit(solution)/shard_map/dot_general | solution.py:317
  145.4 60.6 %experts.4 = (f32[512,16,128]{2,1,0:T(8,128)}, f32[512,16,128]{2,1,0:T(8,128)}, f32[512,16,128]{2,1,0:T(8,128)}, f32[512,16,128]{2,1,0:T(8,128)}) custom-call(s32[32]{0:T(128)} %squeeze.81.count_s, s32[4608]{0:T(1024)} %squeeze.82.tok_s, f32[4608]{0:T(1024)} %squeeze.83.gate_s, bf16[512,16,128]{2,1,0:T(8,128)(2,1)} %collective-permute-done.seg_a, ...), custom_call_target="tpu_custom_call" | custom-call | flops 39862665216 | bytes 138412032 | tf_op jit(solution)/shard_map/experts/pallas_call | solution.py:171
  211.6 45.5 %collective-permute-done.14.seg_a = bf16[512,16,128]{2,1,0:T(8,128)(2,1)S(1)} collective-permute-done((bf16[512,16,128]{2,1,0:T(8,128)(2,1)}, bf16[512,16,128]{2,1,0:T(8,128)(2,1)S(1)}, u32[]{:S(2)}, u32[]{:S(2)}) %collective-permute-start.14) | collective-permute-done | bytes 2097184 | tf_op jit(solution)/shard_map/ppermute | solution.py:295
  260.6 6.1 add.193.refs_1_
  266.7 4.8 add.192.refs_0_
  271.5 61.5 %experts.5 = (f32[512,16,128]{2,1,0:T(8,128)}, f32[512,16,128]{2,1,0:T(8,128)}, f32[512,16,128]{2,1,0:T(8,128)}, f32[512,16,128]{2,1,0:T(8,128)}) custom-call(s32[32]{0:T(128)} %squeeze.90.count_s, s32[4608]{0:T(1024)} %squeeze.91.tok_s, f32[4608]{0:T(1024)} %squeeze.92.gate_s, bf16[512,16,128]{2,1,0:T(8,128)(2,1)} %copy-done.7, ...), custom_call_target="tpu_custom_call" | custom-call | flops 39862665216 | bytes 138412032 | tf_op jit(solution)/shard_map/experts/pallas_call | solution.py:171
  339.7 45.5 %collective-permute-done.10.seg_a = bf16[512,16,128]{2,1,0:T(8,128)(2,1)S(1)} collective-permute-done((bf16[512,16,128]{2,1,0:T(8,128)(2,1)}, bf16[512,16,128]{2,1,0:T(8,128)(2,1)S(1)}, u32[]{:S(2)}, u32[]{:S(2)}) %collective-permute-start.10) | collective-permute-done | bytes 2097184 | tf_op jit(solution)/shard_map/ppermute | solution.py:295
  388.6 6.2 add.195.refs_1_
  394.8 4.7 add.194.refs_0_
  399.5 61.8 %experts.6 = (f32[512,16,128]{2,1,0:T(8,128)}, f32[512,16,128]{2,1,0:T(8,128)}, f32[512,16,128]{2,1,0:T(8,128)}, f32[512,16,128]{2,1,0:T(8,128)}) custom-call(s32[32]{0:T(128)} %squeeze.87.count_s, s32[4608]{0:T(1024)} %squeeze.88.tok_s, f32[4608]{0:T(1024)} %squeeze.89.gate_s, bf16[512,16,128]{2,1,0:T(8,128)(2,1)} %copy-done.8, ...), custom_call_target="tpu_custom_call" | custom-call | flops 39862665216 | bytes 138412032 | tf_op jit(solution)/shard_map/experts/pallas_call | solution.py:171
  466.5 3.9 collective-permute-done.22
  470.8 18.0 %convolution_convert_fusion.refs_0_.refs_2_ = bf16[1024,2048]{1,0:T(8,128)(2,1)} fusion(bf16[1024,2816]{1,0:T(8,128)(2,1)} %multiply_convert_fusion.refs_0_, bf16[2816,2048]{1,0:T(8,128)(2,1)} %param.17), kind=kOutput, calls=%fused_computation.3 | convolution fusion | flops 11813257216 | bytes 21495808 | tf_op jit(solution)/shard_map/dot_general | solution.py:319
  490.8 66.6 %collective-permute-done.23 = f32[512,16,128]{2,1,0:T(8,128)} collective-permute-done((f32[512,16,128]{2,1,0:T(8,128)}, f32[512,16,128]{2,1,0:T(8,128)}, u32[]{:S(2)}, u32[]{:S(2)}) %collective-permute-start.23) | collective-permute-done | bytes 4194336 | tf_op jit(solution)/shard_map/ppermute | solution.py:295
  557.4 7.6 %add_add_fusion.refs_1_ = f32[512,16,128]{2,1,0:T(8,128)} fusion(f32[512,16,128]{2,1,0:T(8,128)} %collective-permute-done.23, f32[512,16,128]{2,1,0:T(8,128)} %get-tuple-element.35, f32[512,16,128]{2,1,0:T(8,128)} %collective-permute-done.22), kind=kLoop, calls=%fused_computation.1 | loop fusion | flops 2097152 | bytes 16777216 | tf_op jit(solution)/shard_map/add | solution.py:336
  567.7 6.3 add_add_fusion.1.refs_0_
  574.0 63.7 %experts.7 = (f32[512,16,128]{2,1,0:T(8,128)}, f32[512,16,128]{2,1,0:T(8,128)}, f32[512,16,128]{2,1,0:T(8,128)}, f32[512,16,128]{2,1,0:T(8,128)}) custom-call(s32[32]{0:T(128)} %squeeze.84.count_s, s32[4608]{0:T(1024)} %squeeze.85.tok_s, f32[4608]{0:T(1024)} %squeeze.86.gate_s, bf16[512,16,128]{2,1,0:T(8,128)(2,1)} %bitcast.99, ...), custom_call_target="tpu_custom_call" | custom-call | flops 39862665216 | bytes 138412032 | tf_op jit(solution)/shard_map/experts/pallas_call | solution.py:171
  639.9 10.1 %collective-permute-done.7.refs_2_ = f32[512,16,128]{2,1,0:T(8,128)} collective-permute-done((f32[512,16,128]{2,1,0:T(8,128)}, f32[512,16,128]{2,1,0:T(8,128)}, u32[]{:S(2)}, u32[]{:S(2)}) %collective-permute-start.7) | collective-permute-done | bytes 4194336 | tf_op jit(solution)/shard_map/ppermute | solution.py:295
  650.0 6.6 collective-permute-done.5.refs_1_
  656.7 10.5 %add_up.2.refs_0_ = f32[1024,2048]{1,0:T(8,128)} custom-call(bf16[1024,2048]{1,0:T(8,128)(2,1)} %convolution_convert_fusion.refs_0_.refs_2_, f32[512,16,128]{2,1,0:T(8,128)} %collective-permute-done.5.refs_1_, f32[512,16,128]{2,1,0:T(8,128)} %collective-permute-done.7.refs_2_), custom_call_target="tpu_custom_call" | custom-call | flops 16777216 | bytes 33554432 | tf_op jit(solution)/shard_map/add_up/pallas_call | solution.py:227
  667.1 72.8 %collective-permute-done.26.refs_5_ = f32[512,16,128]{2,1,0:T(8,128)} collective-permute-done((f32[512,16,128]{2,1,0:T(8,128)}, f32[512,16,128]{2,1,0:T(8,128)}, u32[]{:S(2)}, u32[]{:S(2)}) %collective-permute-start.26) | collective-permute-done | bytes 4194336 | tf_op jit(solution)/shard_map/ppermute | solution.py:295
  739.9 6.6 collective-permute-done.27.refs_6_
  746.5 14.9 %add_up.3 = bf16[1024,2048]{1,0:T(8,128)(2,1)} custom-call(f32[1024,2048]{1,0:T(8,128)} %add_up.2.refs_0_, f32[512,16,128]{2,1,0:T(8,128)} %get-tuple-element.37.refs_1_, f32[512,16,128]{2,1,0:T(8,128)} %get-tuple-element.38.refs_2_, f32[512,16,128]{2,1,0:T(8,128)} %collective-permute-done.24.refs_3_, f32[512,16,128]{2,1,0:T(8,128)} %collective-permute-done.25.refs_4_, ...), custom_call_target="tpu_custom_call" | custom-call | flops 16777216 | bytes 33554432 | tf_op jit(solution)/shard_map/add_up/pallas_call | solution.py:227
  (171 shorter events, 87.5 us)
Async XLA Ops:
  3.4 122.4 %collective-permute-start = (bf16[512,16,128]{2,1,0:T(8,128)(2,1)S(1)}, bf16[512,16,128]{2,1,0:T(8,128)(2,1)}, u32[]{:S(2)}, u32[]{:S(2)}) collective-permute-start(bf16[512,16,128]{2,1,0:T(8,128)(2,1)S(1)} %bitcast.96), channel_id=1, source_target_pairs={{0,2},{1,3},{2,4},{3,5},{4,6},{5,7},{6,0},{7,1},{8,10},{9,11},{10,... | collective-permute-start | bytes 6291464 | tf_op jit(solution)/shard_map/ppermute | solution.py:295
  7.7 118.3 %collective-permute-start.1 = (bf16[512,16,128]{2,1,0:T(8,128)(2,1)}, bf16[512,16,128]{2,1,0:T(8,128)(2,1)}, u32[]{:S(2)}, u32[]{:S(2)}) collective-permute-start(bf16[512,16,128]{2,1,0:T(8,128)(2,1)} %bitcast.50.seg_b), channel_id=1, source_target_pairs={{0,6},{1,7},{2,0},{3,1},{4,2},{5,3},{6,4},{7,5},{8,14},{9,15},{10,... | collective-permute-start | bytes 6291464 | tf_op jit(solution)/shard_map/ppermute | solution.py:295
  125.8 19.6 %collective-permute-start.2 = (bf16[512,16,128]{2,1,0:T(8,128)(2,1)}, bf16[512,16,128]{2,1,0:T(8,128)(2,1)}, u32[]{:S(2)}, u32[]{:S(2)}) collective-permute-start(bf16[512,16,128]{2,1,0:T(8,128)(2,1)} %collective-permute-done.seg_a), channel_id=1, source_target_pairs={{0,1},{1,0},{2,3},{3,2},{4,5},{5,4},{6,7},{7,6},{8,9},{9,8},{10,11... | collective-permute-start | bytes 6291464 | tf_op jit(solution)/shard_map/ppermute | solution.py:295
  126.0 19.5 %collective-permute-start.3 = (bf16[512,16,128]{2,1,0:T(8,128)(2,1)}, bf16[512,16,128]{2,1,0:T(8,128)(2,1)}, u32[]{:S(2)}, u32[]{:S(2)}) collective-permute-start(bf16[512,16,128]{2,1,0:T(8,128)(2,1)} %collective-permute-done.1.seg_b), channel_id=1, source_target_pairs={{0,1},{1,0},{2,3},{3,2},{4,5},{5,4},{6,7},{7,6},{8,9},{9,8},{10,11... | collective-permute-start | bytes 6291464 | tf_op jit(solution)/shard_map/ppermute | solution.py:295
  206.0 54.6 %collective-permute-start.6 = (f32[512,16,128]{2,1,0:T(8,128)}, f32[512,16,128]{2,1,0:T(8,128)}, u32[]{:S(2)}, u32[]{:S(2)}) collective-permute-start(f32[512,16,128]{2,1,0:T(8,128)} %get-tuple-element.28), channel_id=1, source_target_pairs={{0,1},{1,0},{2,3},{3,2},{4,5},{5,4},{6,7},{7,6},{8,9},{9,8},{10,11... | collective-permute-start | bytes 12582920 | tf_op jit(solution)/shard_map/ppermute | solution.py:295
  208.8 57.9 %collective-permute-start.4 = (f32[512,16,128]{2,1,0:T(8,128)}, f32[512,16,128]{2,1,0:T(8,128)}, u32[]{:S(2)}, u32[]{:S(2)}) collective-permute-start(f32[512,16,128]{2,1,0:T(8,128)} %get-tuple-element.26), channel_id=1, source_target_pairs={{0,1},{1,0},{2,3},{3,2},{4,5},{5,4},{6,7},{7,6},{8,9},{9,8},{10,11... | collective-permute-start | bytes 12582920 | tf_op jit(solution)/shard_map/ppermute | solution.py:295
  208.9 48.2 %collective-permute-start.14 = (bf16[512,16,128]{2,1,0:T(8,128)(2,1)}, bf16[512,16,128]{2,1,0:T(8,128)(2,1)S(1)}, u32[]{:S(2)}, u32[]{:S(2)}) collective-permute-start(bf16[512,16,128]{2,1,0:T(8,128)(2,1)} %collective-permute-done.seg_a), channel_id=1, source_target_pairs={{0,2},{1,3},{2,4},{3,5},{4,6},{5,7},{6,0},{7,1},{8,10},{9,11},{10,... | collective-permute-start | bytes 6291464 | tf_op jit(solution)/shard_map/ppermute | solution.py:295
  208.9 49.5 %collective-permute-start.15 = (bf16[512,16,128]{2,1,0:T(8,128)(2,1)}, bf16[512,16,128]{2,1,0:T(8,128)(2,1)}, u32[]{:S(2)}, u32[]{:S(2)}) collective-permute-start(bf16[512,16,128]{2,1,0:T(8,128)(2,1)} %collective-permute-done.1.seg_b), channel_id=1, source_target_pairs={{0,6},{1,7},{2,0},{3,1},{4,2},{5,3},{6,4},{7,5},{8,14},{9,15},{10,... | collective-permute-start | bytes 6291464 | tf_op jit(solution)/shard_map/ppermute | solution.py:295
  333.0 55.6 %collective-permute-start.19 = (f32[512,16,128]{2,1,0:T(8,128)}, f32[512,16,128]{2,1,0:T(8,128)}, u32[]{:S(2)}, u32[]{:S(2)}) collective-permute-start(f32[512,16,128]{2,1,0:T(8,128)} %get-tuple-element.32), channel_id=1, source_target_pairs={{0,1},{1,0},{2,3},{3,2},{4,5},{5,4},{6,7},{7,6},{8,9},{9,8},{10,11... | collective-permute-start | bytes 12582920 | tf_op jit(solution)/shard_map/ppermute | solution.py:295
  336.9 57.9 %collective-permute-start.18 = (f32[512,16,128]{2,1,0:T(8,128)}, f32[512,16,128]{2,1,0:T(8,128)}, u32[]{:S(2)}, u32[]{:S(2)}) collective-permute-start(f32[512,16,128]{2,1,0:T(8,128)} %get-tuple-element.30), channel_id=1, source_target_pairs={{0,1},{1,0},{2,3},{3,2},{4,5},{5,4},{6,7},{7,6},{8,9},{9,8},{10,11... | collective-permute-start | bytes 12582920 | tf_op jit(solution)/shard_map/ppermute | solution.py:295
  337.0 48.2 %collective-permute-start.10 = (bf16[512,16,128]{2,1,0:T(8,128)(2,1)}, bf16[512,16,128]{2,1,0:T(8,128)(2,1)S(1)}, u32[]{:S(2)}, u32[]{:S(2)}) collective-permute-start(bf16[512,16,128]{2,1,0:T(8,128)(2,1)} %bitcast.50.seg_b), channel_id=1, source_target_pairs={{0,2},{1,3},{2,4},{3,5},{4,6},{5,7},{6,0},{7,1},{8,10},{9,11},{10,... | collective-permute-start | bytes 6291464 | tf_op jit(solution)/shard_map/ppermute | solution.py:295
  337.0 49.5 %collective-permute-start.11 = (bf16[512,16,128]{2,1,0:T(8,128)(2,1)}, bf16[512,16,128]{2,1,0:T(8,128)(2,1)}, u32[]{:S(2)}, u32[]{:S(2)}) collective-permute-start(bf16[512,16,128]{2,1,0:T(8,128)(2,1)} %bitcast.97), channel_id=1, source_target_pairs={{0,6},{1,7},{2,0},{3,1},{4,2},{5,3},{6,4},{7,5},{8,14},{9,15},{10,... | collective-permute-start | bytes 6291464 | tf_op jit(solution)/shard_map/ppermute | solution.py:295
  385.2 14.3 %collective-permute-start.12 = (bf16[512,16,128]{2,1,0:T(8,128)(2,1)S(1)}, bf16[512,16,128]{2,1,0:T(8,128)(2,1)}, u32[]{:S(2)}, u32[]{:S(2)}) collective-permute-start(bf16[512,16,128]{2,1,0:T(8,128)(2,1)S(1)} %collective-permute-done.10.seg_a), channel_id=1, source_target_pairs={{0,1},{1,0},{2,3},{3,2},{4,5},{5,4},{6,7},{7,6},{8,9},{9,8},{10,11... | collective-permute-start | bytes 6291464 | tf_op jit(solution)/shard_map/ppermute | solution.py:295
  463.3 110.7 %collective-permute-start.8 = (bf16[512,16,128]{2,1,0:T(8,128)(2,1)}, bf16[512,16,128]{2,1,0:T(8,128)(2,1)}, u32[]{:S(2)}, u32[]{:S(2)}) collective-permute-start(bf16[512,16,128]{2,1,0:T(8,128)(2,1)} %bitcast.98), channel_id=1, source_target_pairs={{0,1},{1,0},{2,3},{3,2},{4,5},{5,4},{6,7},{7,6},{8,9},{9,8},{10,11... | collective-permute-start | bytes 6291464 | tf_op jit(solution)/shard_map/ppermute | solution.py:295
  463.5 110.5 %collective-permute-start.9 = (bf16[512,16,128]{2,1,0:T(8,128)(2,1)}, bf16[512,16,128]{2,1,0:T(8,128)(2,1)}, u32[]{:S(2)}, u32[]{:S(2)}) collective-permute-start(bf16[512,16,128]{2,1,0:T(8,128)(2,1)} %bitcast.50.seg_b), channel_id=1, source_target_pairs={{0,1},{1,0},{2,3},{3,2},{4,5},{5,4},{6,7},{7,6},{8,9},{9,8},{10,11... | collective-permute-start | bytes 6291464 | tf_op jit(solution)/shard_map/ppermute | solution.py:295
  463.8 93.5 %collective-permute-start.23 = (f32[512,16,128]{2,1,0:T(8,128)}, f32[512,16,128]{2,1,0:T(8,128)}, u32[]{:S(2)}, u32[]{:S(2)}) collective-permute-start(f32[512,16,128]{2,1,0:T(8,128)} %add.195.refs_1_), channel_id=1, source_target_pairs={{0,2},{1,3},{2,4},{3,5},{4,6},{5,7},{6,0},{7,1},{8,10},{9,11},{10,... | collective-permute-start | bytes 12582920 | tf_op jit(solution)/shard_map/ppermute | solution.py:295
  463.8 103.8 %collective-permute-start.21 = (f32[512,16,128]{2,1,0:T(8,128)}, f32[512,16,128]{2,1,0:T(8,128)}, u32[]{:S(2)}, u32[]{:S(2)}) collective-permute-start(f32[512,16,128]{2,1,0:T(8,128)} %add.194.refs_0_), channel_id=1, source_target_pairs={{0,6},{1,7},{2,0},{3,1},{4,2},{5,3},{6,4},{7,5},{8,14},{9,15},{10,... | collective-permute-start | bytes 12582920 | tf_op jit(solution)/shard_map/ppermute | solution.py:295
  470.5 94.5 %collective-permute-start.20 = (f32[512,16,128]{2,1,0:T(8,128)}, f32[512,16,128]{2,1,0:T(8,128)}, u32[]{:S(2)}, u32[]{:S(2)}) collective-permute-start(f32[512,16,128]{2,1,0:T(8,128)} %get-tuple-element.34), channel_id=1, source_target_pairs={{0,1},{1,0},{2,3},{3,2},{4,5},{5,4},{6,7},{7,6},{8,9},{9,8},{10,11... | collective-permute-start | bytes 12582920 | tf_op jit(solution)/shard_map/ppermute | solution.py:295
  557.4 92.7 %collective-permute-start.7 = (f32[512,16,128]{2,1,0:T(8,128)}, f32[512,16,128]{2,1,0:T(8,128)}, u32[]{:S(2)}, u32[]{:S(2)}) collective-permute-start(f32[512,16,128]{2,1,0:T(8,128)} %add.193.refs_1_), channel_id=1, source_target_pairs={{0,2},{1,3},{2,4},{3,5},{4,6},{5,7},{6,0},{7,1},{8,10},{9,11},{10,... | collective-permute-start | bytes 12582920 | tf_op jit(solution)/shard_map/ppermute | solution.py:295
  565.0 91.7 %collective-permute-start.5 = (f32[512,16,128]{2,1,0:T(8,128)}, f32[512,16,128]{2,1,0:T(8,128)}, u32[]{:S(2)}, u32[]{:S(2)}) collective-permute-start(f32[512,16,128]{2,1,0:T(8,128)} %add.192.refs_0_), channel_id=1, source_target_pairs={{0,6},{1,7},{2,0},{3,1},{4,2},{5,3},{6,4},{7,5},{8,14},{9,15},{10,... | collective-permute-start | bytes 12582920 | tf_op jit(solution)/shard_map/ppermute | solution.py:295
  567.7 172.2 %collective-permute-start.26 = (f32[512,16,128]{2,1,0:T(8,128)}, f32[512,16,128]{2,1,0:T(8,128)}, u32[]{:S(2)}, u32[]{:S(2)}) collective-permute-start(f32[512,16,128]{2,1,0:T(8,128)} %add_add_fusion.refs_1_), channel_id=1, source_target_pairs={{0,2},{1,3},{2,4},{3,5},{4,6},{5,7},{6,0},{7,1},{8,10},{9,11},{10,... | collective-permute-start | bytes 12582920 | tf_op jit(solution)/shard_map/ppermute | solution.py:295
  637.7 29.4 %collective-permute-start.24 = (f32[512,16,128]{2,1,0:T(8,128)}, f32[512,16,128]{2,1,0:T(8,128)}, u32[]{:S(2)}, u32[]{:S(2)}) collective-permute-start(f32[512,16,128]{2,1,0:T(8,128)} %get-tuple-element.39), channel_id=1, source_target_pairs={{0,1},{1,0},{2,3},{3,2},{4,5},{5,4},{6,7},{7,6},{8,9},{9,8},{10,11... | collective-permute-start | bytes 12582920 | tf_op jit(solution)/shard_map/ppermute | solution.py:295
  639.8 27.3 %collective-permute-start.25 = (f32[512,16,128]{2,1,0:T(8,128)}, f32[512,16,128]{2,1,0:T(8,128)}, u32[]{:S(2)}, u32[]{:S(2)}) collective-permute-start(f32[512,16,128]{2,1,0:T(8,128)} %get-tuple-element.40), channel_id=1, source_target_pairs={{0,1},{1,0},{2,3},{3,2},{4,5},{5,4},{6,7},{7,6},{8,9},{9,8},{10,11... | collective-permute-start | bytes 12582920 | tf_op jit(solution)/shard_map/ppermute | solution.py:295
  650.0 96.5 %collective-permute-start.27 = (f32[512,16,128]{2,1,0:T(8,128)}, f32[512,16,128]{2,1,0:T(8,128)}, u32[]{:S(2)}, u32[]{:S(2)}) collective-permute-start(f32[512,16,128]{2,1,0:T(8,128)} %add_add_fusion.1.refs_0_), channel_id=1, source_target_pairs={{0,6},{1,7},{2,0},{3,1},{4,2},{5,3},{6,4},{7,5},{8,14},{9,15},{10,... | collective-permute-start | bytes 12582920 | tf_op jit(solution)/shard_map/ppermute | solution.py:295
  (20 other events, 558.1 us)
